TPU v7x, 32 devices: a whole 2x2x4 slice. The times are simulated.
32 devices in a mesh: vert: 8 (over z, y), col: 4 (over x, core).
Axes of the slice: x: 2, y: 2, z: 4, core: 2. Of those that a mesh axis runs over, the one named last changes fastest.
Arguments:
- coeffs: bfloat16 [64, 400], P(('vert', 'col')), may hold values from -6 to 6
- shape_basis: bfloat16 [400, 3, 656], P('col', None, 'vert'), may hold values from -0.3125 to 0.3125
- template: float32 [3, 656], P(None, 'vert'), may hold values from -6 to 6
- regressor: float32 [55, 656], P(None, 'vert'), may hold values from -0.5 to 0.5
- quaternions: float32 [64, 4, 55], P(('vert', 'col')), may hold values from -1.5 to 1.5, as said below
- translation: float32 [64, 3], P(('vert', 'col')), may hold values from -6 to 6
- parents: int32 [55], replicated, may hold values from 0 to 53, as said below
- skin_index: int32 [656, 4], P('vert'), may hold values from 0 to 54, all different within a row
- skin_raw: float32 [656, 4], P('vert'), may hold values from 0.1 to 1
Outputs:
- posed_vertices: bfloat16 [64, 3, 656], P(('vert', 'col'))
Inputs may be any that keep to these rules, and one draw needn't show every extreme that they name: parents[0] = 0 and parents[j] < j for j >= 1. `skin_index`: the four joints of a vertex differ. `quaternions`: component 0 lies in [0.5, 1.5].
All inputs are finite; a program needn't handle non-finite values.
Results may differ from a plain program's by a relative error of at most 0.0024.
Values may be sent and summed in bfloat16 or wider, within the bound.
No kernel may reach another device: no remote copies, remote signals or barrier semaphores. Data moves between devices by JAX's collectives and lax.ppermute only.
A program may use at most 64 MiB of HBM per device.

v0:
```python
import jax
import jax.numpy as jnp
from jax import lax
from jax.sharding import PartitionSpec as P


def rotations(quaternions):
    quat_w = jnp.transpose(quaternions[:, 0])
    quat_x = jnp.transpose(quaternions[:, 1])
    quat_y = jnp.transpose(quaternions[:, 2])
    quat_z = jnp.transpose(quaternions[:, 3])
    scale_two = 2.0 / (quat_w * quat_w + quat_x * quat_x + quat_y * quat_y + quat_z * quat_z)
    matrix_rows = [
        [
            1.0 - scale_two * (quat_y * quat_y + quat_z * quat_z),
            scale_two * (quat_x * quat_y - quat_w * quat_z),
            scale_two * (quat_x * quat_z + quat_w * quat_y),
        ],
        [
            scale_two * (quat_x * quat_y + quat_w * quat_z),
            1.0 - scale_two * (quat_x * quat_x + quat_z * quat_z),
            scale_two * (quat_y * quat_z - quat_w * quat_x),
        ],
        [
            scale_two * (quat_x * quat_z - quat_w * quat_y),
            scale_two * (quat_y * quat_z + quat_w * quat_x),
            1.0 - scale_two * (quat_x * quat_x + quat_y * quat_y),
        ],
    ]
    return jnp.stack([jnp.stack(entry, axis=1) for entry in matrix_rows], axis=1)


def kinematics(joints, quaternions, translation, parents):
    joint_total = quaternions.shape[2]
    local_rots = rotations(quaternions)
    places = jnp.transpose(joints, (2, 1, 0))
    glob_rot = jnp.zeros_like(local_rots).at[0].set(local_rots[0])
    glob_pos = jnp.zeros_like(places).at[0].set(places[0] + jnp.transpose(translation))

    def compose(joint, state_pair):
        rot_now, pos_now = state_pair
        parent = lax.dynamic_index_in_dim(parents, joint, 0, keepdims=False)
        parent_rot = lax.dynamic_index_in_dim(rot_now, parent, 0, keepdims=False)
        parent_pos = lax.dynamic_index_in_dim(pos_now, parent, 0, keepdims=False)
        local_rot = lax.dynamic_index_in_dim(local_rots, joint, 0, keepdims=False)
        offset = lax.dynamic_index_in_dim(
            places, joint, 0, keepdims=False
        ) - lax.dynamic_index_in_dim(places, parent, 0, keepdims=False)
        new_rot = jnp.einsum("amc,mbc->abc", parent_rot, local_rot, precision=lax.Precision.HIGHEST)
        new_pos = (
            jnp.einsum("amc,mc->ac", parent_rot, offset, precision=lax.Precision.HIGHEST)
            + parent_pos
        )
        rot_now = lax.dynamic_update_index_in_dim(rot_now, new_rot, joint, 0)
        pos_now = lax.dynamic_update_index_in_dim(pos_now, new_pos, joint, 0)
        return (rot_now, pos_now)

    glob_rot, glob_pos = lax.fori_loop(1, joint_total, compose, (glob_rot, glob_pos))
    correction = glob_pos - jnp.einsum(
        "jamc,jmc->jac", glob_rot, places, precision=lax.Precision.HIGHEST
    )
    frames = jnp.concatenate(
        [glob_rot.reshape(joint_total, 9, glob_rot.shape[3]), correction], axis=1
    )
    return jnp.transpose(frames, (2, 1, 0))


def dense_weights(joint_index, raw_weights, joint_total):
    shares = raw_weights / jnp.sum(raw_weights, axis=1, keepdims=True)
    matches = joint_index[None, :, :] == jnp.arange(joint_total, dtype=jnp.int32)[:, None, None]
    return jnp.sum(
        jnp.where(matches, shares[None, :, :], jnp.zeros_like(shares)[None, :, :]), axis=2
    )


def apply_frames(blended, shaped_wide):
    coords = []
    for axis_out in range(3):
        value = blended[:, 9 + axis_out]
        for axis_in in range(3):
            value = value + blended[:, 3 * axis_out + axis_in] * shaped_wide[:, axis_in]
        coords.append(value)
    return jnp.stack(coords, axis=1)


def body(
    coeffs,
    shape_basis,
    template,
    regressor,
    quaternions,
    translation,
    parents,
    skin_index,
    skin_raw,
):
    joint_total = regressor.shape[0]
    full_basis = lax.all_gather(shape_basis, "col", axis=0, tiled=True)
    components = full_basis.shape[0]
    vert_count = full_basis.shape[2]
    flat_basis = full_basis.reshape(components, 3 * vert_count)
    base_row = template.reshape(1, 3 * vert_count)
    full_shape = (
        jnp.dot(
            lax.all_gather(coeffs, "vert", axis=0, tiled=True),
            flat_basis,
            preferred_element_type=jnp.float32,
        )
        + base_row
    )
    group_count = full_shape.shape[0]
    shaped_three = full_shape.astype(jnp.bfloat16).reshape(group_count, 3, vert_count)
    partial_value = jnp.einsum(
        "cmv,jv->cmj",
        full_shape.reshape(group_count, 3, vert_count),
        regressor,
        precision=lax.Precision.HIGHEST,
    )
    joints = lax.psum_scatter(partial_value, "vert", scatter_dimension=0, tiled=True)
    own_frames = kinematics(joints, quaternions, translation, parents)
    group_frames = lax.all_gather(own_frames, "vert", axis=0, tiled=True)
    weight_grid = dense_weights(skin_index, skin_raw, joint_total)
    blended = jnp.einsum("cej,jv->cev", group_frames, weight_grid, precision=lax.Precision.HIGHEST)
    posed_local = apply_frames(blended, shaped_three.astype(jnp.float32)).astype(jnp.bfloat16)
    return lax.all_to_all(posed_local, "vert", split_axis=0, concat_axis=2, tiled=True)


def solution(mesh):
    in_specs = (
        P(("vert", "col"), None),
        P("col", None, "vert"),
        P(None, "vert"),
        P(None, "vert"),
        P(("vert", "col"), None, None),
        P(("vert", "col"), None),
        P(),
        P("vert", None),
        P("vert", None),
    )
    out_specs = P(("vert", "col"), None, None)
    return jax.shard_map(body, mesh=mesh, in_specs=in_specs, out_specs=out_specs, check_vma=False)
```

profile of v0, /device:TPU:0, one launch (start us, length us, event | category | flops | bytes accessed | tf_op | source)
XLA Modules:
  0.0 288.7 jit_solution(18105276202222392193)
XLA Ops:
  0.0 0.9 multiply_add_fusion.2
  0.9 0.8 add.183
  1.7 28.1 %all-gather = bf16[8,2,400]{2,1,0:T(2,128)(2,1)S(1)} all-gather(bf16[1,2,400]{2,1,0:T(2,128)(2,1)} %bitcast.166), channel_id=1, replica_groups=mesh['vert'=8,'col'=4] {'vert'}, dimensions={0}, use_global_device_ids=true | all-gather | bytes 14400 | tf_op jit(solution)/shard_map/all_gather | solution.py:105
  29.9 6.5 %all_gather.10 = bf16[400,3,82]{2,1,0:T(4,128)(2,1)S(1)} all-gather(bf16[100,3,82]{2,1,0:T(4,128)(2,1)S(1)} %copy.86), channel_id=1, replica_groups=mesh['vert'=8,'col'=4] {'col'}, dimensions={0}, use_global_device_ids=true | all-gather | bytes 246000 | tf_op jit(solution)/shard_map/all_gather | solution.py:98
  38.1 35.4 %all-reduce.1 = f32[16,3,55]{2,0,1:T(8,128)S(1)} all-reduce(f32[16,3,55]{2,0,1:T(8,128)S(1)} %fusion.8), channel_id=2, replica_groups=mesh['vert'=8,'col'=4] {'vert'}, use_global_device_ids=true, to_apply=%region_0.0.clone | all-reduce | flops 2640 | bytes 21120
  73.6 0.7 copy-done.8
  77.1 169.4 %while.19 = (s32[]{:T(128)}, f32[55,3,3,2]{2,3,1,0:T(2,128)S(1)}, f32[55,3,2]{1,2,0:T(2,128)S(1)}, f32[55,3,3,2]{2,3,1,0:T(2,128)S(1)}, s32[55]{0:T(128)S(1)}, /...) while((s32[]{:T(128)}, f32[55,3,3,2]{2,3,1,0:T(2,128)S(1)}, ...), condition=%wide.region_2.0_spmd, body=%wide.region_1.0_spmd.sunk | while | flops 884 | bytes 9465 | solution.py:58
  80.2 0.7 dynamic_slice.89
  83.3 0.7 dynamic_slice.89
  86.5 0.6 dynamic_slice.89
  89.6 0.7 dynamic_slice.89
  95.9 0.7 dynamic_slice.89
  102.2 0.7 dynamic_slice.89
  105.3 0.7 dynamic_slice.89
  108.4 0.6 dynamic_slice.89
  111.6 0.7 dynamic_slice.89
  117.8 0.7 dynamic_slice.89
  124.1 0.7 dynamic_slice.89
  127.3 0.7 dynamic_slice.89
  130.4 0.7 dynamic_slice.89
  133.5 0.7 dynamic_slice.89
  139.8 0.7 dynamic_slice.89
  146.1 0.7 dynamic_slice.89
  152.4 0.7 dynamic_slice.89
  155.5 0.7 dynamic_slice.89
  158.6 0.6 dynamic_slice.89
  161.8 0.7 dynamic_slice.89
  168.0 0.7 dynamic_slice.89
  174.3 0.7 dynamic_slice.89
  177.5 0.7 dynamic_slice.89
  180.6 0.7 dynamic_slice.89
  183.7 0.7 dynamic_slice.89
  190.0 0.7 dynamic_slice.89
  196.3 0.7 dynamic_slice.89
  202.6 0.7 dynamic_slice.89
  205.7 0.7 dynamic_slice.89
  208.8 0.6 dynamic_slice.89
  212.0 0.7 dynamic_slice.89
  218.2 0.7 dynamic_slice.89
  224.5 0.7 dynamic_slice.89
  227.7 0.7 dynamic_slice.89
  230.8 0.7 dynamic_slice.89
  233.9 0.7 dynamic_slice.89
  240.2 0.7 dynamic_slice.89
  247.3 30.5 %all_gather.11 = f32[16,12,55]{2,1,0:T(8,128)S(1)} all-gather(f32[2,12,55]{2,1,0:T(8,128)S(1)} %copy.95), channel_id=1, replica_groups=mesh['vert'=8,'col'=4] {'vert'}, dimensions={0}, use_global_device_ids=true | all-gather | bytes 47520 | tf_op jit(solution)/shard_map/all_gather | solution.py:121
  277.9 0.7 copy-done.4
  279.0 8.9 %all_to_all.18 = bf16[8,2,246]{2,1,0:T(2,128)(2,1)S(1)} all-to-all(bf16[8,2,246]{2,1,0:T(2,128)(2,1)S(1)} %reshape.121), channel_id=1, replica_groups=mesh['vert'=8,'col'=4] {'vert'}, dimensions={0} | all-to-all | bytes 15744 | tf_op jit(solution)/shard_map/all_to_all | solution.py:125
  288.0 0.7 all_to_all.16
  (559 shorter events, 48.4 us)
Async XLA Ops:
  0.0 38.0 %copy-start = (f32[55,82]{1,0:T(8,128)S(1)}, f32[55,82]{1,0:T(8,128)}, u32[]{:S(2)}) copy-start(f32[55,82]{1,0:T(8,128)} %param.18) | copy-start | bytes 54124
  0.0 0.9 copy-start.2
  0.0 29.8 %copy-start.1 = (bf16[100,3,82]{0,2,1:T(8,128)(2,1)S(1)}, bf16[100,3,82]{0,2,1:T(8,128)(2,1)}, u32[]{:S(2)}) copy-start(bf16[100,3,82]{0,2,1:T(8,128)(2,1)} %param.16) | copy-start | bytes 147604
  37.0 0.7 copy-start.6
  73.6 0.7 copy-start.8
  75.7 0.7 copy-start.5
  76.4 0.7 copy-start.7
  247.3 30.6 %copy-start.3 = (f32[82,4]{0,1:T(4,128)S(1)}, f32[82,4]{0,1:T(4,128)}, u32[]{:S(2)}) copy-start(f32[82,4]{0,1:T(4,128)} %param.23) | copy-start | bytes 3940
  277.9 0.7 copy-start.4
where the time goes:
time: 291 us; the launch traced here: 289 us
  blocking collectives  109 us (37%)
  loops' own time  102 us (35%)
  local copies, waits for them, and re-layouts  54.8 us (19%)
  matrix products  19.3 us (7%)
    another operation x1, loops' own time, kinematics(): lax.fori_loop(1, joint_total, compose, (glob_rot, glob_pos))  102 us
    unnamed x1, blocking collectives  35.4 us
    dynamic_slice x54, local copies, waits for them, and re-layouts, compose(): parent = lax.dynamic_index_in_dim(parents, joint, 0, keepdims=False)  35.1 us
    all_gather x1, blocking collectives, body(): group_frames = lax.all_gather(own_frames, 'vert', axis=0, tiled=True)  30.5 us
    all_gather x1, blocking collectives, body(): lax.all_gather(coeffs, 'vert', axis=0, tiled=True)  28.1 us
    dot_general x54, matrix products, compose(): jnp.einsum('amc,mbc->abc', parent_rot, local_rot, precision=lax.Precision...  11.1 us
    all_to_all x1, blocking collectives, body(): lax.all_to_all(posed_local, 'vert', split_axis=0, concat_axis=2, tiled=True)  8.89 us
    dot_general x54, matrix products, compose(): jnp.einsum('amc,mc->ac', parent_rot, offset, precision=lax.Precision.HIGH...  7.68 us

commit v1 on v0

v1 whole, which is shorter than its diff:
```python
import functools

import jax
import jax.numpy as jnp
from jax import lax
from jax.experimental import pallas as pl
from jax.experimental.pallas import tpu as pltpu
from jax.sharding import PartitionSpec as P

LANES = 128
SUBS = 8
VMEM = pl.BlockSpec(memory_space=pltpu.VMEM)


def round_up(value, step):
    return -(-value // step) * step


def pack_kernel(groups, spans, slots, coeffs_ref, index_ref, raw_ref, out_ref):
    own_chars, comps = coeffs_ref.shape
    block = comps // groups
    verts = index_ref.shape[1]
    rows = out_ref.shape[1]
    column = lax.axis_index("col")
    wide = coeffs_ref[...].astype(jnp.float32)
    index = index_ref[...].astype(jnp.float32)
    raw = raw_ref[...]
    out_ref[...] = jnp.zeros_like(out_ref)
    per_group = slots // groups
    picked = []
    for which in range(per_group):
        slot = column * per_group + which
        sel = lax.broadcasted_iota(jnp.int32, index.shape, 0) == slot
        picked.append(jnp.sum(jnp.where(sel, index, 0.0), axis=0, keepdims=True))
        picked.append(jnp.sum(jnp.where(sel, raw, 0.0), axis=0, keepdims=True))
    for group in range(groups):
        piece = wide[:, group * block : (group + 1) * block]
        for span in range(spans):
            out_ref[span * groups + group, 0:own_chars, 0:block] = piece
            for row, value in enumerate(picked):
                out_ref[span * groups + group, own_chars + row : own_chars + row + 1, 0:verts] = value


def split_two(value):
    high = value.astype(jnp.bfloat16)
    return high, (value - high.astype(jnp.float32)).astype(jnp.bfloat16)


def across(lhs, rhs):
    return lax.dot_general(
        lhs, rhs, (((1,), (1,)), ((), ())), preferred_element_type=jnp.float32
    )


def shape_kernel(
    own_chars, groups, recv_ref, basis_ref, template_ref, regressor_ref, out_ref, basis_s, template_s, reg_s
):
    _, verts, block = basis_ref.shape
    joints = regressor_ref.shape[0]
    start = round_up(verts, SUBS)
    first = LANES - start
    rest = joints - first
    step = round_up(rest, SUBS)
    rows_in = recv_ref.shape[0]
    basis_s[...] = jnp.zeros_like(basis_s)
    for coord in range(3):
        basis_s[coord, 0:verts, 0:block] = basis_ref[coord]
    template_s[...] = jnp.zeros_like(template_s)
    template_s[0:3, 0:verts] = template_ref[...] * (1.0 / groups)
    reg_s[...] = jnp.zeros_like(reg_s)
    reg_s[start:LANES, 0:verts] = regressor_ref[0:first, :]
    reg_s[LANES : LANES + rest, 0:verts] = regressor_ref[first:joints, :]
    reg_high, reg_low = split_two(reg_s[...])
    reg_all = jnp.concatenate([reg_high, reg_low, reg_high], axis=1)
    per_source = recv_ref.shape[1]
    chunk = min(32, rows_in)

    def do_chunk(number):
        base = number * chunk
        coeffs = jnp.concatenate(
            [recv_ref[pl.ds(base, chunk), char, :] for char in range(own_chars)], axis=0
        ).astype(jnp.bfloat16)
        total = own_chars * chunk
        shapes = [
            across(coeffs, basis_s[coord]) + template_s[coord : coord + 1, :] for coord in range(3)
        ]
        stacked = jnp.concatenate(shapes, axis=0)
        high, low = split_two(stacked)
        sums = across(jnp.concatenate([high, high, low], axis=1), reg_all)
        last = jnp.zeros((total, LANES), jnp.float32)
        for coord in range(3):
            mine = sums[coord * total : (coord + 1) * total]
            extra = mine[:, LANES:]
            if coord:
                extra = pltpu.roll(extra, coord * step, 1)
            last = last + extra
            row = shapes[coord] + mine[:, :LANES]
            for char in range(own_chars):
                out_ref[pl.ds(base, chunk), 4 * char + coord, :] = row[char * chunk : (char + 1) * chunk]
        for char in range(own_chars):
            out_ref[pl.ds(base, chunk), 4 * char + 3, :] = last[char * chunk : (char + 1) * chunk]

    if rows_in == chunk:
        do_chunk(0)
    else:
        lax.fori_loop(0, rows_in // chunk, lambda number, carry: (do_chunk(number), carry)[1], 0)


def pick(table, index):
    return jnp.take_along_axis(table, index, axis=1, mode="promise_in_bounds")


def pose_kernel(
    groups, verts, skin_ref, recv_ref, quat_ref, shift_ref, parents_ref, out_ref, quat_s, parent_s, shift_s, sum_s, flat_s
):
    own_chars, _, joints = quat_ref.shape
    spans = recv_ref.shape[0] // groups
    half = SUBS // own_chars
    start = round_up(verts, SUBS)
    first = LANES - start
    step = round_up(joints - first, SUBS)
    lane = lax.broadcasted_iota(jnp.int32, (SUBS, LANES), 1)
    sub = lax.broadcasted_iota(jnp.int32, (SUBS, LANES), 0)

    def by_char(rows):
        value = jnp.broadcast_to(rows[0], (SUBS, LANES))
        for char in range(1, own_chars):
            value = jnp.where(sub >= char * half, rows[char], value)
        return value

    quat_s[...] = jnp.zeros_like(quat_s)
    quat_s[:, 0:1, :] = jnp.ones_like(quat_s[:, 0:1, :])
    quat_s[:, :, 0:joints] = quat_ref[...]
    quat = [by_char([quat_s[char, comp : comp + 1, :] for char in range(own_chars)]) for comp in range(4)]
    w, x, y, z = quat
    two = 2.0 / (w * w + x * x + y * y + z * z)
    rot = [
        [1.0 - two * (y * y + z * z), two * (x * y - w * z), two * (x * z + w * y)],
        [two * (x * y + w * z), 1.0 - two * (x * x + z * z), two * (y * z - w * x)],
        [two * (x * z - w * y), two * (y * z + w * x), 1.0 - two * (x * x + y * y)],
    ]
    parent_s[...] = jnp.zeros_like(parent_s)
    parent_s[0:1, 0:joints] = parents_ref[...]
    parent = jnp.broadcast_to(parent_s[0:1, :], (SUBS, LANES))
    above = jnp.where((lane >= joints) | (lane == 0), joints, parent)
    shift_s[...] = jnp.zeros_like(shift_s)
    shift_s[0:own_chars, 0:3] = shift_ref[...]
    shift = by_char([shift_s[char : char + 1, :] for char in range(own_chars)])

    total = None
    for span in range(spans):
        value = recv_ref[span * groups]
        for group in range(1, groups):
            value = value + recv_ref[span * groups + group]
        sum_s[span * SUBS : (span + 1) * SUBS, :] = value
        total = value if total is None else total + value
    places = []
    for coord in range(3):
        near = pltpu.roll(total, LANES - start, 1)
        far = pltpu.roll(total, (first - coord * step) % LANES, 1)
        near = by_char([near[4 * char + coord : 4 * char + coord + 1, :] for char in range(own_chars)])
        far = by_char([far[4 * char + 3 : 4 * char + 4, :] for char in range(own_chars)])
        places.append(jnp.where(lane < first, near, far))

    move = []
    for coord in range(3):
        origin = shift if coord == 0 else pltpu.roll(shift, LANES - coord, 1)
        offset = jnp.where(lane == 0, places[coord] + origin, places[coord] - pick(places[coord], parent))
        move.append(jnp.where(lane < joints, offset, 0.0))
    for level in range(max(1, (joints - 1).bit_length())):
        up = [[pick(rot[a][b], above) for b in range(3)] for a in range(3)]
        up_move = [pick(move[a], above) for a in range(3)]
        new_rot = [
            [up[a][0] * rot[0][b] + up[a][1] * rot[1][b] + up[a][2] * rot[2][b] for b in range(3)]
            for a in range(3)
        ]
        move = [
            up[a][0] * move[0] + up[a][1] * move[1] + up[a][2] * move[2] + up_move[a] for a in range(3)
        ]
        rot = new_rot
        above = pick(above, above)
    frames = [rot[a][b] for a in range(3) for b in range(3)]
    for a in range(3):
        frames.append(
            move[a] - (rot[a][0] * places[0] + rot[a][1] * places[1] + rot[a][2] * places[2])
        )

    slots = groups * ((skin_ref.shape[1] - own_chars) // 2)
    per_group = slots // groups
    for base in range(0, spans, SUBS):
        count = min(SUBS, spans - base)
        index, weight = [], []
        for slot in range(slots):
            group, which = slot // per_group, slot % per_group
            row = own_chars + 2 * which
            index.append(
                jnp.concatenate(
                    [skin_ref[(base + s) * groups + group, row : row + 1, :] for s in range(count)]
                    + [jnp.zeros((SUBS - count, LANES), jnp.float32)] * (count < SUBS),
                    axis=0,
                ).astype(jnp.int32)
            )
            weight.append(
                jnp.concatenate(
                    [skin_ref[(base + s) * groups + group, row + 1 : row + 2, :] for s in range(count)]
                    + [jnp.zeros((SUBS - count, LANES), jnp.float32)] * (count < SUBS),
                    axis=0,
                )
            )
        norm = functools.reduce(lambda p, q: p + q, weight)
        scale = 1.0 / jnp.where(norm > 0.0, norm, 1.0)
        weight = [value * scale for value in weight]
        for char in range(own_chars):
            blend = []
            for entry in range(12):
                table = jnp.broadcast_to(
                    frames[entry][char * half : char * half + 1, :], (SUBS, LANES)
                )
                value = weight[0] * pick(table, index[0])
                for slot in range(1, slots):
                    value = value + weight[slot] * pick(table, index[slot])
                blend.append(value)
            shaped = [
                jnp.concatenate(
                    [
                        sum_s[(base + s) * SUBS + 4 * char + coord : (base + s) * SUBS + 4 * char + coord + 1, :]
                        for s in range(count)
                    ]
                    + [jnp.zeros((SUBS - count, LANES), jnp.float32)] * (count < SUBS),
                    axis=0,
                )
                .astype(jnp.bfloat16)
                .astype(jnp.float32)
                for coord in range(3)
            ]
            for a in range(3):
                value = blend[9 + a]
                for m in range(3):
                    value = value + blend[3 * a + m] * shaped[m]
                for s in range(count):
                    low = (base + s) * verts
                    flat_s[a * own_chars + char : a * own_chars + char + 1, low : low + verts] = value[
                        s : s + 1, 0:verts
                    ]
    for a in range(3):
        out_ref[a] = flat_s[a * own_chars : (a + 1) * own_chars, :].astype(jnp.bfloat16)


def body(spans, groups, coeffs, shape_basis, template, regressor, quaternions, translation, parents, skin_index, skin_raw):
    own_chars, _ = coeffs.shape
    verts, slots = skin_index.shape
    joints = regressor.shape[0]
    devices = spans * groups
    rows = own_chars + 2 * slots // groups
    message = pl.pallas_call(
        functools.partial(pack_kernel, groups, spans, slots),
        out_shape=jax.ShapeDtypeStruct((devices, rows, LANES), jnp.float32),
        in_specs=[VMEM] * 3,
        out_specs=VMEM,
        name="pack",
    )(coeffs, skin_index.T, skin_raw.T)
    first_recv = lax.all_to_all(message, ("vert", "col"), 0, 0, tiled=True)
    partials = pl.pallas_call(
        functools.partial(shape_kernel, own_chars, groups),
        out_shape=jax.ShapeDtypeStruct((devices, 4 * own_chars, LANES), jnp.float32),
        in_specs=[VMEM] * 4,
        out_specs=VMEM,
        scratch_shapes=[
            pltpu.VMEM((3, LANES, LANES), jnp.bfloat16),
            pltpu.VMEM((SUBS, LANES), jnp.float32),
            pltpu.VMEM((2 * LANES, LANES), jnp.float32),
        ],
        name="shape",
    )(first_recv, shape_basis.transpose(1, 2, 0), template, regressor)
    second_recv = lax.all_to_all(partials, ("vert", "col"), 0, 0, tiled=True)
    posed = pl.pallas_call(
        functools.partial(pose_kernel, groups, verts),
        out_shape=jax.ShapeDtypeStruct((3, own_chars, spans * verts), jnp.bfloat16),
        in_specs=[VMEM] * 5,
        out_specs=VMEM,
        scratch_shapes=[
            pltpu.VMEM((own_chars, 4, LANES), jnp.float32),
            pltpu.VMEM((SUBS, LANES), jnp.int32),
            pltpu.VMEM((SUBS, LANES), jnp.float32),
            pltpu.VMEM((spans * SUBS, LANES), jnp.float32),
            pltpu.VMEM((SUBS, spans * verts), jnp.float32),
        ],
        name="pose",
    )(first_recv, second_recv, quaternions, translation, parents.reshape(1, joints))
    return posed.transpose(1, 0, 2)


def solution(mesh):
    in_specs = (
        P(("vert", "col"), None),
        P("col", None, "vert"),
        P(None, "vert"),
        P(None, "vert"),
        P(("vert", "col"), None, None),
        P(("vert", "col"), None),
        P(),
        P("vert", None),
        P("vert", None),
    )
    out_specs = P(("vert", "col"), None, None)
    return jax.shard_map(
        functools.partial(body, mesh.shape["vert"], mesh.shape["col"]),
        mesh=mesh,
        in_specs=in_specs,
        out_specs=out_specs,
        check_vma=False,
    )
```

time: 291 us -> 32.6 us (0.11)
  loops' own time: 102 us -> 0 us
  blocking collectives: 109 us -> 26.3 us
  local copies, waits for them, and re-layouts: 54.8 us -> 0 us
  matrix products: 19.3 us -> 0 us
  Pallas kernels: 0 us -> 6.01 us
    another operation x1 -> x0, loops' own time: 102 us -> none  [kinematics(): lax.fori_loop(1, joint_total, compose, (glob_rot, glob_pos))]
    all_gather x3 -> x0, blocking collectives: 65.1 us -> none  [the longest x1 30.5 us: body(): group_frames = lax.all_gather(own_frames, 'vert', axis=0, tiled=True)]
    unnamed x1 -> x0, blocking collectives: 35.4 us -> none
    dynamic_slice x54 -> x0, local copies, waits for them, and re-layouts: 35.1 us -> none  [compose(): parent = lax.dynamic_index_in_dim(parents, joint, 0, keepdims=False)]
    dot_general x111 -> x0, matrix products: 19.3 us -> none  [the longest x54 11.1 us: compose(): jnp.einsum('amc,mbc->abc', parent_rot, local_rot, precision=lax.Precision...]
    all_to_all x1 -> x2, blocking collectives: 8.89 us -> 26.3 us  [the longest x1 14.8 us: body(): first_recv = lax.all_to_all(message, ('vert', 'col'), 0, 0, tiled=True)]
    pallas_call x0 -> x3, Pallas kernels: none -> 6.01 us  [the longest x1 2.62 us: body(): pl.pallas_call(functools.partial(pose_kernel, groups, verts), out_shape=j...]
    squeeze x108 -> x0, local copies, waits for them, and re-layouts: 5.97 us -> none  [compose(): parent_rot = lax.dynamic_index_in_dim(rot_now, parent, 0, keepdims=False)]
where the time goes in v1:
time: 32.6 us; the launch traced here: 32.3 us
  blocking collectives  26.3 us (81%)
  Pallas kernels  6.01 us (18%)
    all_to_all x1, blocking collectives, body(): first_recv = lax.all_to_all(message, ('vert', 'col'), 0, 0, tiled=True)  14.8 us
    all_to_all x1, blocking collectives, body(): second_recv = lax.all_to_all(partials, ('vert', 'col'), 0, 0, tiled=True)  11.5 us
    pallas_call x1, Pallas kernels, body(): pl.pallas_call(functools.partial(pose_kernel, groups, verts), out_shape=j...  2.62 us
    pallas_call x1, Pallas kernels, body(): pl.pallas_call(functools.partial(shape_kernel, own_chars, groups), out_sh...  1.98 us
    pallas_call x1, Pallas kernels, body(): pl.pallas_call(functools.partial(pack_kernel, groups, spans, slots), out_...  1.41 us

profile of v1, /device:TPU:0, one launch (start us, length us, event | category | flops | bytes accessed | tf_op | source)
XLA Modules:
  0.0 32.3 jit_solution(2125284767139945087)
XLA Ops:
  0.0 1.4 %pack.1 = f32[32,4,128]{2,1,0:T(4,128)} custom-call(bf16[2,400]{1,0:T(2,128)(2,1)} %coeffs_ref.1, s32[4,82]{1,0:T(4,128)} %bitcast.6, f32[4,82]{1,0:T(4,128)} %bitcast.7), custom_call_target="tpu_custom_call" | custom-call | tf_op jit(solution)/shard_map/pack/pallas_call | solution.py:255
  1.4 14.8 %all_to_all.10.recv_ref.skin_ref = f32[32,4,128]{2,1,0:T(4,128)} all-to-all(f32[32,4,128]{2,1,0:T(4,128)} %pack.1), channel_id=1, replica_groups=mesh['vert'=8,'col'=4] {'vert','col'}, dimensions={0} | all-to-all | bytes 131072 | tf_op jit(solution)/shard_map/all_to_all | solution.py:262
  16.3 2.0 %shape.1 = f32[32,8,128]{2,1,0:T(8,128)} custom-call(f32[32,4,128]{2,1,0:T(4,128)} %all_to_all.10.recv_ref.skin_ref, bf16[3,82,100]{2,1,0:T(8,128)(2,1)} %bitcast.5, f32[3,82]{1,0:T(4,128)} %template_ref.1, f32[55,82]{1,0:T(8,128)} %regressor_ref.1), custom_call_target="tpu_custom_call" | custom-call | tf_op jit(solution)/shard_map/shape/pallas_call | solution.py:263
  18.2 11.5 %all_to_all.11.recv_ref = f32[32,8,128]{2,1,0:T(8,128)} all-to-all(f32[32,8,128]{2,1,0:T(8,128)} %shape.1), channel_id=1, replica_groups=mesh['vert'=8,'col'=4] {'vert','col'}, dimensions={0} | all-to-all | bytes 262144 | tf_op jit(solution)/shard_map/all_to_all | solution.py:275
  29.7 2.6 %pose.1 = bf16[3,2,656]{2,1,0:T(2,128)(2,1)} custom-call(f32[32,4,128]{2,1,0:T(4,128)} %all_to_all.10.recv_ref.skin_ref, f32[32,8,128]{2,1,0:T(8,128)} %all_to_all.11.recv_ref, f32[2,4,55]{2,1,0:T(4,128)} %quat_ref.1, f32[2,3]{1,0:T(2,128)} %shift_ref.1, s32[1,55]{1,0:T(1,128)} %bitcast.8), custom_call_target="tpu_custom_call" | custom-call | tf_op jit(solution)/shard_map/pose/pallas_call | solution.py:276

commit v2 on v0

v2 whole, which is shorter than its diff:
```python
import functools

import jax
import jax.numpy as jnp
from jax import lax
from jax.experimental import pallas as pl
from jax.experimental.pallas import tpu as pltpu
from jax.sharding import PartitionSpec as P

LANES = 128
SUBS = 8
VMEM = pl.BlockSpec(memory_space=pltpu.VMEM)
HBM = pl.BlockSpec(memory_space=pltpu.HBM)
F32 = jnp.float32
BF16 = jnp.bfloat16


def round_up(value, step):
    return -(-value // step) * step


def layout(verts, joints):
    start = round_up(verts, SUBS)
    first = LANES - start
    rest = joints - first
    step = round_up(rest, SUBS)
    return start, first, rest, step


def in_hbm(*values):
    return [pltpu.with_memory_space_constraint(value, pltpu.HBM) for value in values]


def split_two(value):
    high = value.astype(BF16)
    return high, (value - high.astype(F32)).astype(BF16)


def dot(lhs, rhs):
    return jnp.dot(lhs, rhs, preferred_element_type=F32)


def each(count, limit, step):
    if count <= limit:
        for number in range(count):
            step(number)
    else:
        lax.fori_loop(0, count, lambda number, carry: (step(number), carry)[1], 0)


def dot_across(lhs, rhs):
    return lax.dot_general(lhs, rhs, (((1,), (1,)), ((), ())), preferred_element_type=F32)


def pick(table, index):
    return jnp.take_along_axis(table, index, axis=1, mode="promise_in_bounds")


def fetch(pairs, sems):
    copies = [pltpu.make_async_copy(src, dst, sems.at[n]) for n, (src, dst) in enumerate(pairs)]
    for copy in copies:
        copy.start()
    return copies


def pack_kernel(groups, spans, coeffs_hbm, index_hbm, raw_hbm, *refs):
    passed = (len(refs) - 5) // 2
    sources, out_ref, targets = refs[:passed], refs[passed], refs[passed + 1 : 2 * passed + 1]
    coeffs_s, index_s, raw_s, sems = refs[2 * passed + 1 :]
    copies = fetch(
        [(coeffs_hbm, coeffs_s), (index_hbm, index_s), (raw_hbm, raw_s), *zip(sources, targets)], sems
    )
    own_chars, comps = coeffs_s.shape
    block = comps // groups
    slots, verts = index_s.shape
    per_group = slots // groups
    column = lax.axis_index("col")
    out_ref[...] = jnp.zeros_like(out_ref)
    for copy in copies[:3]:
        copy.wait()
    wide = coeffs_s[...].astype(F32)
    index = index_s[...].astype(F32)
    raw = raw_s[...]
    picked = []
    for which in range(per_group):
        sel = lax.broadcasted_iota(jnp.int32, index.shape, 0) == column * per_group + which
        picked.append(jnp.sum(jnp.where(sel, index, 0.0), axis=0, keepdims=True))
        picked.append(jnp.sum(jnp.where(sel, raw, 0.0), axis=0, keepdims=True))
    for group in range(groups):
        piece = wide[:, group * block : (group + 1) * block]
        for span in range(spans):
            out_ref[span * groups + group, 0:own_chars, 0:block] = piece
            for row, value in enumerate(picked):
                at = own_chars + row
                out_ref[span * groups + group, at : at + 1, 0:verts] = value
    for copy in copies[3:]:
        copy.wait()


def shape_kernel(
    groups,
    recv_ref,
    basis_ref,
    template_ref,
    regressor_ref,
    quat_ref,
    move_ref,
    parents_ref,
    out_ref,
    diff_ref,
    shift_ref,
    coef_ref,
    weight_ref,
    pad_s,
    temp_s,
    reg_s,
    quat_s,
    parent_s,
    skin_s,
):
    _, verts, block = basis_ref.shape
    own_chars, _, joints = quat_ref.shape
    count = recv_ref.shape[0]
    spans = count // groups
    slots = skin_s.shape[0] // 2
    tiles = skin_s.shape[1] // LANES
    start, first, rest, step = layout(verts, joints)
    lane = lax.broadcasted_iota(jnp.int32, (SUBS, LANES), 1)
    sub = lax.broadcasted_iota(jnp.int32, (SUBS, LANES), 0)
    row = sub // own_chars

    pad_s[...] = jnp.zeros_like(pad_s)
    for coord in range(3):
        pad_s[coord, 0:verts, 0:block] = basis_ref[coord]
    temp_s[...] = jnp.zeros_like(temp_s)
    temp_s[0:3, 0:verts] = template_ref[...] * (1.0 / groups)
    reg_s[...] = jnp.zeros_like(reg_s)
    reg_s[start:LANES, 0:verts] = regressor_ref[0:first, :]
    reg_s[LANES : LANES + rest, 0:verts] = regressor_ref[first:joints, :]
    reg_high, reg_low = split_two(reg_s[...])
    reg_all = jnp.concatenate([reg_high, reg_low, reg_high], axis=1)
    chunk = min(32, count)
    total = own_chars * chunk

    def do_chunk(number):
        at = pl.ds(number * chunk, chunk)
        coeffs = jnp.concatenate([recv_ref[at, char, :] for char in range(own_chars)], axis=0).astype(BF16)
        shapes = [dot_across(coeffs, pad_s[coord]) + temp_s[coord : coord + 1, :] for coord in range(3)]
        high, low = split_two(jnp.concatenate(shapes, axis=0))
        sums = dot_across(jnp.concatenate([high, high, low], axis=1), reg_all)
        last = sums[0:total, LANES:]
        for coord in range(1, 3):
            last = last + pltpu.roll(sums[coord * total : (coord + 1) * total, LANES:], coord * step, 1)
        rows = [shapes[coord] + sums[coord * total : (coord + 1) * total, :LANES] for coord in range(3)]
        for place, value in enumerate(rows + [last]):
            for char in range(own_chars):
                out_ref[at, place * own_chars + char, :] = value[char * chunk : (char + 1) * chunk]

    each(count // chunk, 1, do_chunk)

    def by_char(rows):
        value = jnp.broadcast_to(rows[0], (SUBS, LANES))
        for char in range(1, own_chars):
            value = jnp.where(sub % own_chars == char, rows[char], value)
        return value

    quat_s[...] = jnp.zeros_like(quat_s)
    quat_s[:, 0:1, :] = jnp.ones_like(quat_s[:, 0:1, :])
    quat_s[:, :, 0:joints] = quat_ref[...]
    w, x, y, z = [
        by_char([quat_s[char, comp : comp + 1, :] for char in range(own_chars)]) for comp in range(4)
    ]
    two = 2.0 / (w * w + x * x + y * y + z * z)
    rot = [
        [1.0 - two * (y * y + z * z), two * (x * y - w * z), two * (x * z + w * y)],
        [two * (x * y + w * z), 1.0 - two * (x * x + z * z), two * (y * z - w * x)],
        [two * (x * z - w * y), two * (y * z + w * x), 1.0 - two * (x * x + y * y)],
    ]
    parent_s[...] = jnp.zeros_like(parent_s)
    parent_s[0:1, 0:joints] = parents_ref[...]
    parent = jnp.broadcast_to(parent_s[0:1, :], (SUBS, LANES))
    parent = jnp.where((lane >= joints) | (lane == 0), joints, parent)

    spot = lax.broadcasted_iota(jnp.int32, (LANES, LANES), 0)
    target = lax.broadcasted_iota(jnp.int32, (LANES, LANES), 1)
    inner = spot % step
    of_spot = jnp.where(
        spot >= start, spot - start, jnp.where((spot < 3 * step) & (inner < rest), first + inner, -1)
    )
    chain = jnp.where(of_spot == target, 1.0, 0.0)
    above = parent
    for _ in range(max(1, (joints - 1).bit_length())):
        up = [[pick(rot[a][b], above) for b in range(3)] for a in range(3)]
        rot = [
            [up[a][0] * rot[0][b] + up[a][1] * rot[1][b] + up[a][2] * rot[2][b] for b in range(3)]
            for a in range(3)
        ]
        chain = jnp.concatenate(
            [chain[n : n + SUBS] + pick(chain[n : n + SUBS], above) for n in range(0, LANES, SUBS)],
            axis=0,
        )
        above = pick(above, above)
    chain = chain.astype(BF16)

    tables = []
    for turn in range(3):
        value = rot[2][(2 + turn) % 3]
        for a in (1, 0):
            value = jnp.where(row == a, rot[a][(a + turn) % 3], value)
        tables.append(value)
    for a in range(3):
        value = jnp.zeros((SUBS, LANES), F32)
        for coord in range(3):
            diff = pick(rot[a][coord], parent) - rot[a][coord]
            near = pltpu.roll(diff, start, 1)
            far = pltpu.roll(diff, (coord * step - first) % LANES, 1)
            value = jnp.where((row == coord) & (lane >= start), near, value)
            value = jnp.where(
                (row == 3) & (lane >= coord * step) & (lane < coord * step + rest), far, value
            )
        diff_ref[a] = value
    moved = jnp.zeros((SUBS, LANES), F32)
    for char in range(own_chars):
        for a in range(3):
            moved = jnp.where(sub == a * own_chars + char, move_ref[char : char + 1, a : a + 1], moved)
    shift_ref[...] = moved

    skin_s[...] = jnp.zeros_like(skin_s)
    for span in range(spans):
        rows = jnp.concatenate(
            [recv_ref[span * groups + group, own_chars:, :] for group in range(groups)], axis=0
        )
        skin_s[:, span * verts : (span + 1) * verts] = rows[:, :verts]

    def do_tile(number, tables, chain):
        if isinstance(number, int):
            at = slice(number * LANES, (number + 1) * LANES)
        else:
            at = pl.ds(pl.multiple_of(number * LANES, LANES), LANES)
        skin = skin_s[:, at]
        index = [skin[2 * n : 2 * n + 1].astype(jnp.int32) for n in range(slots)]
        share = [skin[2 * n + 1 : 2 * n + 2] for n in range(slots)]
        norm = functools.reduce(lambda p, q: p + q, share)
        scale = 1.0 / jnp.where(norm > 0.0, norm, 1.0)
        share = [value * scale for value in share]
        wide = [jnp.broadcast_to(value, (SUBS, LANES)) for value in index]
        for turn in range(3):
            coef_ref[turn, :, at] = functools.reduce(
                lambda p, q: p + q, [share[n] * pick(tables[turn], wide[n]) for n in range(slots)]
            )
        grid = jnp.zeros((LANES, LANES), F32)
        for n in range(slots):
            grid = jnp.where(spot == index[n], share[n], grid)
        high, low = split_two(grid)
        closed = dot(chain, high) + dot(chain, low)
        high, low = split_two(closed)
        weight_ref[0:LANES, at] = high
        weight_ref[LANES : 2 * LANES, at] = low

    if tiles <= 8:
        for number in range(tiles):
            do_tile(number, tables, chain)
    else:
        carry = (tuple(tables), chain)
        lax.fori_loop(0, tiles, lambda number, kept: (do_tile(number, *kept), kept)[1], carry)


def pose_kernel(groups, own_chars, verts, recv_ref, diff_ref, shift_ref, coef_ref, weight_ref, out_ref):
    spans = recv_ref.shape[0] // groups
    width = out_ref.shape[2]
    tiles = coef_ref.shape[2] // LANES
    lane = lax.broadcasted_iota(jnp.int32, (SUBS, LANES), 1)
    sub = lax.broadcasted_iota(jnp.int32, (SUBS, LANES), 0)
    row = sub // own_chars
    total = None
    shapes = [None] * tiles
    for span in range(spans):
        value = recv_ref[span * groups]
        for group in range(1, groups):
            value = value + recv_ref[span * groups + group]
        total = value if total is None else total + value
        low = span * verts
        turned = pltpu.roll(value, low % LANES, 1) if low % LANES else value
        for tile in range(low // LANES, (low + verts - 1) // LANES + 1):
            begin = low - tile * LANES
            shapes[tile] = turned if begin <= 0 else jnp.where(lane >= begin, turned, shapes[tile])

    terms = []
    for a in range(3):
        term = diff_ref[a] * total
        step = own_chars
        while step < SUBS:
            term = term + pltpu.roll(term, step, 0)
            step *= 2
        terms.append(term)
    lhs = jnp.where(row == 0, terms[0], jnp.where(row == 1, terms[1], jnp.where(row == 2, terms[2], 0.0)))
    high = lhs.astype(BF16).astype(F32)
    left = jnp.concatenate([high, lhs - high], axis=0).astype(BF16)
    right = jnp.concatenate([high, jnp.zeros_like(high)], axis=0).astype(BF16)
    moved = dot(jnp.concatenate([left, right], axis=1), weight_ref[...])
    moved = moved[:SUBS] + moved[SUBS:]
    for tile in range(tiles):
        at = slice(tile * LANES, (tile + 1) * LANES)
        shape = shapes[tile].astype(BF16).astype(F32)
        by_one = pltpu.roll(shape, own_chars, 0)
        by_two = pltpu.roll(shape, 2 * own_chars, 0)
        by_three = pltpu.roll(shape, 3 * own_chars, 0)
        posed = (
            moved[:, at]
            + shift_ref[...]
            + coef_ref[0, :, at] * shape
            + coef_ref[1, :, at] * jnp.where(row < 2, by_three, by_two)
            + coef_ref[2, :, at] * jnp.where(row < 1, by_two, by_one)
        )
        end = min(width, (tile + 1) * LANES)
        for a in range(3):
            out_ref[a, :, tile * LANES : end] = posed[
                a * own_chars : (a + 1) * own_chars, : end - tile * LANES
            ].astype(BF16)


def body(spans, groups, coeffs, shape_basis, template, regressor, quaternions, translation, parents, skin_index, skin_raw):
    own_chars, comps = coeffs.shape
    verts, slots = skin_index.shape
    joints = regressor.shape[0]
    devices = spans * groups
    rows = own_chars + 2 * slots // groups
    padded = round_up(spans * verts, LANES)
    whole = jax.ShapeDtypeStruct
    room = pltpu.CompilerParams(vmem_limit_bytes=16 * 2**20)
    local = [
        shape_basis.transpose(1, 2, 0),
        template,
        regressor,
        quaternions,
        translation,
        parents.reshape(1, joints),
    ]
    message, *local = pl.pallas_call(
        functools.partial(pack_kernel, groups, spans),
        out_shape=[whole((devices, rows, LANES), F32)] + [whole(value.shape, value.dtype) for value in local],
        in_specs=[HBM] * (3 + len(local)),
        out_specs=[VMEM] * (1 + len(local)),
        scratch_shapes=[
            pltpu.VMEM((own_chars, comps), BF16),
            pltpu.VMEM((slots, verts), jnp.int32),
            pltpu.VMEM((slots, verts), F32),
            pltpu.SemaphoreType.DMA((3 + len(local),)),
        ],
        compiler_params=room,
        name="pack",
    )(*in_hbm(coeffs, skin_index.T, skin_raw.T, *local))
    received = lax.all_to_all(message, ("vert", "col"), 0, 0, tiled=True)
    partials, diff, shift, coef, weight = pl.pallas_call(
        functools.partial(shape_kernel, groups),
        out_shape=[
            whole((devices, 4 * own_chars, LANES), F32),
            whole((3, SUBS, LANES), F32),
            whole((SUBS, LANES), F32),
            whole((3, SUBS, padded), F32),
            whole((2 * LANES, padded), BF16),
        ],
        in_specs=[VMEM] * 7,
        out_specs=[VMEM] * 5,
        scratch_shapes=[
            pltpu.VMEM((3, LANES, LANES), BF16),
            pltpu.VMEM((SUBS, LANES), F32),
            pltpu.VMEM((2 * LANES, LANES), F32),
            pltpu.VMEM((own_chars, 4, LANES), F32),
            pltpu.VMEM((SUBS, LANES), jnp.int32),
            pltpu.VMEM((2 * slots, padded), F32),
        ],
        compiler_params=room,
        name="shape",
    )(received, *local)
    received = lax.all_to_all(partials, ("vert", "col"), 0, 0, tiled=True)
    posed = pl.pallas_call(
        functools.partial(pose_kernel, groups, own_chars, verts),
        out_shape=whole((3, own_chars, spans * verts), BF16),
        in_specs=[VMEM] * 5,
        out_specs=VMEM,
        compiler_params=room,
        name="pose",
    )(received, diff, shift, coef, weight)
    return posed.transpose(1, 0, 2)


def solution(mesh):
    in_specs = (
        P(("vert", "col"), None),
        P("col", None, "vert"),
        P(None, "vert"),
        P(None, "vert"),
        P(("vert", "col"), None, None),
        P(("vert", "col"), None),
        P(),
        P("vert", None),
        P("vert", None),
    )
    out_specs = P(("vert", "col"), None, None)
    return jax.shard_map(
        functools.partial(body, mesh.shape["vert"], mesh.shape["col"]),
        mesh=mesh,
        in_specs=in_specs,
        out_specs=out_specs,
        check_vma=False,
    )
```

time: 291 us -> 27.6 us (0.09)
  loops' own time: 102 us -> 0 us
  blocking collectives: 109 us -> 24.5 us
  local copies, waits for them, and re-layouts: 54.8 us -> 0 us
  matrix products: 19.3 us -> 0 us
  Pallas kernels: 0 us -> 2.97 us
    another operation x1 -> x0, loops' own time: 102 us -> none  [kinematics(): lax.fori_loop(1, joint_total, compose, (glob_rot, glob_pos))]
    all_gather x3 -> x0, blocking collectives: 65.1 us -> none  [the longest x1 30.5 us: body(): group_frames = lax.all_gather(own_frames, 'vert', axis=0, tiled=True)]
    unnamed x1 -> x0, blocking collectives: 35.4 us -> none
    dynamic_slice x54 -> x0, local copies, waits for them, and re-layouts: 35.1 us -> none  [compose(): parent = lax.dynamic_index_in_dim(parents, joint, 0, keepdims=False)]
    dot_general x111 -> x0, matrix products: 19.3 us -> none  [the longest x54 11.1 us: compose(): jnp.einsum('amc,mbc->abc', parent_rot, local_rot, precision=lax.Precision...]
    all_to_all x1 -> x2, blocking collectives: 8.89 us -> 24.5 us  [the longest x1 14.5 us: body(): received = lax.all_to_all(message, ('vert', 'col'), 0, 0, tiled=True)]
    squeeze x108 -> x0, local copies, waits for them, and re-layouts: 5.97 us -> none  [compose(): parent_rot = lax.dynamic_index_in_dim(rot_now, parent, 0, keepdims=False)]
    transpose x55 -> x0, local copies, waits for them, and re-layouts: 5.49 us -> none  [the longest x54 5.49 us: compose(): jnp.einsum('amc,mbc->abc', parent_rot, local_rot, precision=lax.Precision...]
where the time goes in v2:
time: 27.6 us; the launch traced here: 27.4 us
  blocking collectives  24.5 us (89%)
  Pallas kernels  2.97 us (11%)
    all_to_all x1, blocking collectives, body(): received = lax.all_to_all(message, ('vert', 'col'), 0, 0, tiled=True)  14.5 us
    all_to_all x1, blocking collectives, body(): received = lax.all_to_all(partials, ('vert', 'col'), 0, 0, tiled=True)  9.91 us
    pallas_call x1, Pallas kernels, body(): pl.pallas_call(functools.partial(shape_kernel, groups), out_shape=[whole(...  1.16 us
    pallas_call x1, Pallas kernels, body(): pl.pallas_call(functools.partial(pack_kernel, groups, spans), out_shape=[...  1.02 us
    pallas_call x1, Pallas kernels, body(): pl.pallas_call(functools.partial(pose_kernel, groups, own_chars, verts),...  0.79 us

profile of v2, /device:TPU:0, one launch (start us, length us, event | category | flops | bytes accessed | tf_op | source)
XLA Modules:
  0.0 27.4 jit_solution(9455422951379775199)
XLA Ops:
  0.0 1.0 %pack.1 = (f32[32,4,128]{2,1,0:T(4,128)S(1)}, bf16[3,82,100]{2,1,0:T(8,128)(2,1)S(1)}, f32[3,82]{1,0:T(4,128)S(1)}, f32[55,82]{1,0:T(8,128)S(1)}, f32[2,4,55]{2,...) custom-call(bf16[2,400]{1,0:T(2,128)(2,1)} %coeffs_hbm.1, s32[4,82]{1,0:T(4,128)} %bitcast.6, f32[4,82]{1,0:T(4,128)} %bitcast.7, ...), custom_call_target="tpu_custom_call" | custom-call | tf_op jit(solution)/shard_map/pack/pallas_call | solution.py:339
  1.0 14.5 %all_to_all.10.recv_ref = f32[32,4,128]{2,1,0:T(4,128)S(1)} all-to-all(f32[32,4,128]{2,1,0:T(4,128)S(1)} %get-tuple-element.17), channel_id=1, replica_groups=mesh['vert'=8,'col'=4] {'vert','col'}, dimensions={0} | all-to-all | bytes 131072 | tf_op jit(solution)/shard_map/all_to_all | solution.py:353
  15.6 1.2 %shape.1 = (f32[32,8,128]{2,1,0:T(8,128)S(1)}, f32[3,8,128]{2,1,0:T(8,128)S(1)}, f32[8,128]{1,0:T(8,128)S(1)}, f32[3,8,768]{2,1,0:T(8,128)S(1)}, bf16[256,768]{1,0:T(8,128)(2,1)S(1)}) custom-call(f32[32,4,128]{2,1,0:T(4,128)S(1)} %all_to_all.10.recv_ref, bf16[3,82,100]{2,1,0:T(8,128)(2,1)S(1)} %get-tuple-element.18.basis_ref, ...), custom_call_target="tpu_custom_call" | custom-call | tf_op jit(solution)/shard_map/shape/pallas_call | solution.py:354
  16.7 9.9 %all_to_all.11.recv_ref = f32[32,8,128]{2,1,0:T(8,128)S(1)} all-to-all(f32[32,8,128]{2,1,0:T(8,128)S(1)} %get-tuple-element.24), channel_id=1, replica_groups=mesh['vert'=8,'col'=4] {'vert','col'}, dimensions={0} | all-to-all | bytes 262144 | tf_op jit(solution)/shard_map/all_to_all | solution.py:376
  26.6 0.8 %pose.1 = bf16[3,2,656]{2,1,0:T(2,128)(2,1)} custom-call(f32[32,8,128]{2,1,0:T(8,128)S(1)} %all_to_all.11.recv_ref, f32[3,8,128]{2,1,0:T(8,128)S(1)} %get-tuple-element.25.diff_ref, f32[8,128]{1,0:T(8,128)S(1)} %get-tuple-element.26.shift_ref, f32[3,8,768]{2,1,0:T(8,128)S(1)} %get-tuple-element.27.coef_ref, bf16[256,768]{1,0:T(8,128)(2,1)S(1)} %get-tuple-element.28.weight_ref), custom_call_target="tpu_custom_call" | custom-call | tf_op jit(solution)/shard_map/pose/pallas_call | solution.py:377

commit v3 on v2

v3 whole, which is shorter than its diff:
```python
import functools
import math

import jax
import jax.numpy as jnp
from jax import lax
from jax.experimental import pallas as pl
from jax.experimental.pallas import tpu as pltpu
from jax.sharding import PartitionSpec as P

LANES = 128
SUBS = 8
VMEM = pl.BlockSpec(memory_space=pltpu.VMEM)
HBM = pl.BlockSpec(memory_space=pltpu.HBM)
F32 = jnp.float32
BF16 = jnp.bfloat16


def round_up(value, step):
    return -(-value // step) * step


def layout(verts, joints):
    start = round_up(verts, SUBS)
    first = LANES - start
    rest = joints - first
    step = round_up(rest, SUBS)
    return start, first, rest, step


def in_hbm(*values):
    return [pltpu.with_memory_space_constraint(value, pltpu.HBM) for value in values]


def split_two(value):
    high = value.astype(BF16)
    return high, (value - high.astype(F32)).astype(BF16)


def sum_of(values):
    return functools.reduce(lambda p, q: p + q, values)


def dot(lhs, rhs):
    return jnp.dot(lhs, rhs, preferred_element_type=F32)


def each(count, limit, step):
    if count <= limit:
        for number in range(count):
            step(number)
    else:
        lax.fori_loop(0, count, lambda number, carry: (step(number), carry)[1], 0)


def dot_across(lhs, rhs):
    return lax.dot_general(lhs, rhs, (((1,), (1,)), ((), ())), preferred_element_type=F32)


def pick(table, index):
    return jnp.take_along_axis(table, index, axis=1, mode="promise_in_bounds")


def fetch(pairs, sems):
    copies = [pltpu.make_async_copy(src, dst, sems.at[n]) for n, (src, dst) in enumerate(pairs)]
    for copy in copies:
        copy.start()
    return copies


def coder(verts, block):
    shape = block * 6.0 * 0.3125 + 6.0
    limit = max(shape, verts * 0.5 * shape)
    unit = 2.0**-16
    rate = math.log1p(limit / unit) / 32766.0
    return unit, rate


def pack_kernel(groups, spans, coeffs_hbm, index_hbm, raw_hbm, *refs):
    passed = (len(refs) - 6) // 2
    sources, out_ref, targets = refs[:passed], refs[passed], refs[passed + 1 : 2 * passed + 1]
    coeffs_s, index_s, raw_s, row_s, sems = refs[2 * passed + 1 :]
    copies = fetch(
        [(coeffs_hbm, coeffs_s), (index_hbm, index_s), (raw_hbm, raw_s), *zip(sources, targets)], sems
    )
    own_chars, comps = coeffs_s.shape
    block = comps // groups
    slots, verts = index_s.shape
    per_group = slots // groups
    column = lax.axis_index("col")
    row_s[...] = jnp.zeros_like(row_s)
    for copy in copies[:3]:
        copy.wait()
    wide = coeffs_s[...].astype(F32)
    index = index_s[...].astype(F32)
    raw = raw_s[...]
    for which in range(per_group):
        sel = lax.broadcasted_iota(jnp.int32, index.shape, 0) == column * per_group + which
        at = own_chars + 2 * which
        for more, value in enumerate((index, raw)):
            value = jnp.sum(jnp.where(sel, value, 0.0), axis=0, keepdims=True)
            for group in range(groups):
                row_s[group, at + more : at + more + 1, 0:verts] = value
    for group in range(groups):
        row_s[group, 0:own_chars, 0:block] = wide[:, group * block : (group + 1) * block]
    for group in range(groups):
        value = row_s[group]
        for span in range(spans):
            out_ref[span * groups + group] = value
    for copy in copies[3:]:
        copy.wait()


def shape_kernel(
    groups,
    recv_ref,
    basis_ref,
    template_ref,
    regressor_ref,
    quat_ref,
    move_ref,
    parents_ref,
    out_ref,
    table_ref,
    diff_ref,
    above_ref,
    shift_ref,
    index_ref,
    share_ref,
    pad_s,
    temp_s,
    reg_s,
    quat_s,
    parent_s,
    skin_s,
    sum_s,
):
    _, verts, block = basis_ref.shape
    own_chars, _, joints = quat_ref.shape
    count = recv_ref.shape[0]
    spans = count // groups
    slots = index_ref.shape[0]
    start, first, rest, step = layout(verts, joints)
    lane = lax.broadcasted_iota(jnp.int32, (SUBS, LANES), 1)
    sub = lax.broadcasted_iota(jnp.int32, (SUBS, LANES), 0)
    row = sub // own_chars
    char_of = sub % own_chars

    def by_char(rows):
        value = jnp.broadcast_to(rows[0], (SUBS, LANES))
        for char in range(1, own_chars):
            value = jnp.where(char_of == char, rows[char], value)
        return value

    def by_row(values):
        value = values[-1]
        for n in range(len(values) - 2, -1, -1):
            value = jnp.where(row == n, values[n], value)
        return value

    pad_s[...] = jnp.zeros_like(pad_s)
    for coord in range(3):
        pad_s[coord, 0:verts, 0:block] = basis_ref[coord]
    temp_s[...] = jnp.zeros_like(temp_s)
    temp_s[0:3, 0:verts] = template_ref[...] * (1.0 / groups)
    reg_s[...] = jnp.zeros_like(reg_s)
    reg_s[start:LANES, 0:verts] = regressor_ref[0:first, :]
    reg_s[LANES : LANES + rest, 0:verts] = regressor_ref[first:joints, :]
    reg_high, reg_low = split_two(reg_s[...])
    reg_all = jnp.concatenate([reg_high, reg_low, reg_high], axis=1)
    chunk = min(32, count)
    total = own_chars * chunk
    unit, rate = coder(verts, block)

    def do_chunk(number):
        at = pl.ds(number * chunk, chunk)
        coeffs = jnp.concatenate([recv_ref[at, char, :] for char in range(own_chars)], axis=0).astype(BF16)
        shapes = [dot_across(coeffs, pad_s[coord]) + temp_s[coord : coord + 1, :] for coord in range(3)]
        high, low = split_two(jnp.concatenate(shapes, axis=0))
        sums = dot_across(jnp.concatenate([high, high, low], axis=1), reg_all)
        last = sums[0:total, LANES:]
        for coord in range(1, 3):
            last = last + pltpu.roll(sums[coord * total : (coord + 1) * total, LANES:], coord * step, 1)
        rows = [shapes[coord] + sums[coord * total : (coord + 1) * total, :LANES] for coord in range(3)]
        for place, value in enumerate(rows + [last]):
            code = jnp.log(1.0 + jnp.abs(value) * (1.0 / unit)) * (1.0 / rate)
            code = jnp.where(value < 0.0, -code, code)
            for char in range(own_chars):
                sum_s[:, place * own_chars + char, :] = code[char * chunk : (char + 1) * chunk]
        out_ref[at] = jnp.round(sum_s[...]).astype(jnp.int32).astype(jnp.int16)

    each(count // chunk, 1, do_chunk)

    quat_s[...] = jnp.zeros_like(quat_s)
    quat_s[:, 0:1, :] = jnp.ones_like(quat_s[:, 0:1, :])
    quat_s[:, :, 0:joints] = quat_ref[...]
    w, x, y, z = [
        by_char([quat_s[char, comp : comp + 1, :] for char in range(own_chars)]) for comp in range(4)
    ]
    two = 2.0 / (w * w + x * x + y * y + z * z)
    rot = [
        by_row([1.0 - two * (y * y + z * z), two * (x * y + w * z), two * (x * z - w * y)]),
        by_row([two * (x * y - w * z), 1.0 - two * (x * x + z * z), two * (y * z + w * x)]),
        by_row([two * (x * z + w * y), two * (y * z - w * x), 1.0 - two * (x * x + y * y)]),
    ]
    parent_s[...] = jnp.zeros_like(parent_s)
    parent_s[0:1, 0:joints] = parents_ref[...]
    parent = jnp.broadcast_to(parent_s[0:1, :], (SUBS, LANES))
    parent = jnp.where((lane >= joints) | (lane == 0), joints, parent)

    wide = round_up(joints, SUBS)
    spot = lax.broadcasted_iota(jnp.int32, (wide, LANES), 0)
    target = lax.broadcasted_iota(jnp.int32, (wide, LANES), 1)
    chain = jnp.where((spot == target) & (target < joints), 1.0, 0.0)
    chain = [chain[n : n + SUBS] for n in range(0, wide, SUBS)]
    above = parent
    levels = max(1, (joints - 1).bit_length())
    for level in range(levels):
        spread = []
        for b in range(3):
            turned = [rot[b]] + [pltpu.roll(rot[b], n * own_chars, 0) for n in range(1, 4)]
            spread.append([by_row([turned[(r - m) % 4] for r in range(3)]) for m in range(3)])
        up = [pick(rot[b], above) for b in range(3)]
        rot = [sum_of([up[m] * spread[b][m] for m in range(3)]) for b in range(3)]
        chain = [value + pick(value, above) for value in chain]
        if level + 1 < levels:
            above = pick(above, above)

    for turn in range(3):
        table_ref[turn] = by_row([rot[(a + turn) % 3] for a in range(3)])
    far = jnp.zeros((SUBS, LANES), F32)
    for coord in range(3):
        diff = pick(rot[coord], parent) - rot[coord]
        diff_ref[coord] = jnp.where(lane >= start, pltpu.roll(diff, start, 1), 0.0)
        turned = pltpu.roll(diff, (coord * step - first) % LANES, 1)
        far = jnp.where((lane >= coord * step) & (lane < coord * step + rest), turned, far)
    diff_ref[3] = far
    none = jnp.zeros((SUBS, LANES), F32)
    tail = chain[first // SUBS :]
    tail = tail + [none] * (step // SUBS - len(tail))
    body = chain[: first // SUBS]
    middle = [none] * ((start - 3 * step) // SUBS)
    above_ref[...] = jnp.concatenate(tail * 3 + middle + body, axis=0).astype(BF16)
    moved = none
    for char in range(own_chars):
        for a in range(3):
            moved = jnp.where(sub == a * own_chars + char, move_ref[char : char + 1, a : a + 1], moved)
    shift_ref[...] = moved

    for span in range(spans):
        for group in range(groups):
            value = recv_ref[span * groups + group, own_chars:, :]
            rows = value.shape[0]
            skin_s[group * rows : (group + 1) * rows, span * verts : (span + 1) * verts] = value[:, :verts]
    norm = sum_of([skin_s[2 * n + 1 : 2 * n + 2, :] for n in range(slots)])
    scale = 1.0 / norm
    index_ref[...] = jnp.zeros_like(index_ref)
    share_ref[...] = jnp.zeros_like(share_ref)
    for n in range(slots):
        index_ref[n : n + 1, : spans * verts] = skin_s[2 * n : 2 * n + 1, :].astype(jnp.int32)
        share_ref[n : n + 1, : spans * verts] = skin_s[2 * n + 1 : 2 * n + 2, :] * scale


def pose_kernel(
    groups,
    own_chars,
    verts,
    block,
    recv_ref,
    table_ref,
    diff_ref,
    above_ref,
    shift_ref,
    index_ref,
    share_ref,
    out_ref,
    total_s,
):
    spans = recv_ref.shape[0] // groups
    slots = index_ref.shape[0]
    width = out_ref.shape[2]
    tiles = -(-width // LANES)
    lane = lax.broadcasted_iota(jnp.int32, (SUBS, LANES), 1)
    sub = lax.broadcasted_iota(jnp.int32, (SUBS, LANES), 0)
    row = sub // own_chars
    char_of = sub % own_chars
    unit, rate = coder(verts, block)

    def decode(number):
        code = recv_ref[number].astype(jnp.int32).astype(F32)
        value = jnp.exp(jnp.abs(code) * rate) * unit - unit
        return jnp.where(code < 0.0, -value, value)

    total = None
    shapes = [None] * tiles
    for span in range(spans):
        value = sum_of([decode(span * groups + group) for group in range(groups)])
        total = value if total is None else total + value
        low = span * verts
        turned = pltpu.roll(value, low % LANES, 1) if low % LANES else value
        for tile in range(low // LANES, (low + verts - 1) // LANES + 1):
            begin = low - tile * LANES
            shapes[tile] = turned if begin <= 0 else jnp.where(lane >= begin, turned, shapes[tile])

    total_s[...] = total
    terms = []
    for coord in range(4):
        pair = jnp.broadcast_to(total_s[coord * own_chars : coord * own_chars + 1, :], (SUBS, LANES))
        for char in range(1, own_chars):
            at = coord * own_chars + char
            pair = jnp.where(char_of == char, total_s[at : at + 1, :], pair)
        terms.append(diff_ref[coord] * pair)
    lhs = (terms[0] + terms[1]) + (terms[2] + terms[3])
    high = lhs.astype(BF16).astype(F32)
    moved = dot(jnp.concatenate([high, lhs - high], axis=0).astype(BF16), above_ref[...])
    moved = (moved[:SUBS] + moved[SUBS:]) + shift_ref[...]
    tables = [table_ref[turn] for turn in range(3)]
    for tile in range(tiles):
        end = min(width, (tile + 1) * LANES)
        at = slice(tile * LANES, (tile + 1) * LANES)
        index = [jnp.broadcast_to(index_ref[n : n + 1, at], (SUBS, LANES)) for n in range(slots)]
        share = [share_ref[n : n + 1, at] for n in range(slots)]

        def blend(table):
            return sum_of([share[n] * pick(table, index[n]) for n in range(slots)])

        shape = shapes[tile].astype(BF16).astype(F32)
        by_one = pltpu.roll(shape, own_chars, 0)
        by_two = pltpu.roll(shape, 2 * own_chars, 0)
        by_three = pltpu.roll(shape, 3 * own_chars, 0)
        turned = (
            blend(tables[0]) * shape
            + blend(tables[1]) * jnp.where(row < 2, by_three, by_two)
            + blend(tables[2]) * jnp.where(row < 1, by_two, by_one)
        )
        posed = turned + blend(moved)
        for a in range(3):
            out_ref[a, :, tile * LANES : end] = posed[
                a * own_chars : (a + 1) * own_chars, : end - tile * LANES
            ].astype(BF16)


def body(spans, groups, coeffs, shape_basis, template, regressor, quaternions, translation, parents, skin_index, skin_raw):
    own_chars, comps = coeffs.shape
    verts, slots = skin_index.shape
    joints = regressor.shape[0]
    devices = spans * groups
    block = comps // groups
    rows = own_chars + 2 * slots // groups
    padded = round_up(spans * verts, LANES)
    whole = jax.ShapeDtypeStruct
    room = pltpu.CompilerParams(vmem_limit_bytes=16 * 2**20)
    local = [
        shape_basis.transpose(1, 2, 0),
        template,
        regressor,
        quaternions,
        translation,
        parents.reshape(1, joints),
    ]
    message, *local = pl.pallas_call(
        functools.partial(pack_kernel, groups, spans),
        out_shape=[whole((devices, rows, LANES), F32)] + [whole(value.shape, value.dtype) for value in local],
        in_specs=[HBM] * (3 + len(local)),
        out_specs=[VMEM] * (1 + len(local)),
        scratch_shapes=[
            pltpu.VMEM((own_chars, comps), BF16),
            pltpu.VMEM((slots, verts), jnp.int32),
            pltpu.VMEM((slots, verts), F32),
            pltpu.VMEM((groups, rows, LANES), F32),
            pltpu.SemaphoreType.DMA((3 + len(local),)),
        ],
        compiler_params=room,
        name="pack",
    )(*in_hbm(coeffs, skin_index.T, skin_raw.T, *local))
    received = lax.all_to_all(message, ("vert", "col"), 0, 0, tiled=True)
    partials, *local = pl.pallas_call(
        functools.partial(shape_kernel, groups),
        out_shape=[
            whole((devices, 4 * own_chars, LANES), jnp.int16),
            whole((3, SUBS, LANES), F32),
            whole((4, SUBS, LANES), F32),
            whole((LANES, LANES), BF16),
            whole((SUBS, LANES), F32),
            whole((slots, padded), jnp.int32),
            whole((slots, padded), F32),
        ],
        in_specs=[VMEM] * 7,
        out_specs=[VMEM] * 7,
        scratch_shapes=[
            pltpu.VMEM((3, LANES, LANES), BF16),
            pltpu.VMEM((SUBS, LANES), F32),
            pltpu.VMEM((2 * LANES, LANES), F32),
            pltpu.VMEM((own_chars, 4, LANES), F32),
            pltpu.VMEM((SUBS, LANES), jnp.int32),
            pltpu.VMEM((2 * slots, spans * verts), F32),
            pltpu.VMEM((min(32, devices), 4 * own_chars, LANES), F32),
        ],
        compiler_params=room,
        name="shape",
    )(received, *local)
    received = lax.all_to_all(partials, ("vert", "col"), 0, 0, tiled=True)
    posed = pl.pallas_call(
        functools.partial(pose_kernel, groups, own_chars, verts, block),
        out_shape=whole((3, own_chars, spans * verts), BF16),
        in_specs=[VMEM] * 7,
        out_specs=VMEM,
        scratch_shapes=[pltpu.VMEM((SUBS, LANES), F32)],
        compiler_params=room,
        name="pose",
    )(received, *local)
    return posed.transpose(1, 0, 2)


def solution(mesh):
    in_specs = (
        P(("vert", "col"), None),
        P("col", None, "vert"),
        P(None, "vert"),
        P(None, "vert"),
        P(("vert", "col"), None, None),
        P(("vert", "col"), None),
        P(),
        P("vert", None),
        P("vert", None),
    )
    out_specs = P(("vert", "col"), None, None)
    return jax.shard_map(
        functools.partial(body, mesh.shape["vert"], mesh.shape["col"]),
        mesh=mesh,
        in_specs=in_specs,
        out_specs=out_specs,
        check_vma=False,
    )
```

time: 27.6 us -> 26.5 us (0.960)
  blocking collectives: 24.5 us -> 23.6 us
    all_to_all x1, blocking collectives: 9.91 us -> 9.1 us  [body(): received = lax.all_to_all(partials, ('vert', 'col'), 0, 0, tiled=True)]
    pallas_call x1, Pallas kernels: 1.16 us -> 0.7 us  [body(): pl.pallas_call(functools.partial(shape_kernel, groups), out_shape=[whole(...]
where the time goes in v3:
time: 26.5 us; the launch traced here: 26.4 us
  blocking collectives  23.6 us (89%)
  Pallas kernels  2.7 us (10%)
    all_to_all x1, blocking collectives, body(): received = lax.all_to_all(message, ('vert', 'col'), 0, 0, tiled=True)  14.5 us
    all_to_all x1, blocking collectives, body(): received = lax.all_to_all(partials, ('vert', 'col'), 0, 0, tiled=True)  9.1 us
    pallas_call x1, Pallas kernels, body(): pl.pallas_call(functools.partial(pack_kernel, groups, spans), out_shape=[...  1.02 us
    pallas_call x1, Pallas kernels, body(): pl.pallas_call(functools.partial(pose_kernel, groups, own_chars, verts, b...  0.98 us
    pallas_call x1, Pallas kernels, body(): pl.pallas_call(functools.partial(shape_kernel, groups), out_shape=[whole(...  0.7 us

profile of v3, /device:TPU:0, one launch (start us, length us, event | category | flops | bytes accessed | tf_op | source)
XLA Modules:
  0.0 26.4 jit_solution(15335660966258452294)
XLA Ops:
  0.0 1.0 %pack.1 = (f32[32,4,128]{2,1,0:T(4,128)S(1)}, bf16[3,82,100]{2,1,0:T(8,128)(2,1)S(1)}, f32[3,82]{1,0:T(4,128)S(1)}, f32[55,82]{1,0:T(8,128)S(1)}, f32[2,4,55]{2,...) custom-call(bf16[2,400]{1,0:T(2,128)(2,1)} %coeffs_hbm.1, s32[4,82]{1,0:T(4,128)} %bitcast.6, f32[4,82]{1,0:T(4,128)} %bitcast.7, ...), custom_call_target="tpu_custom_call" | custom-call | tf_op jit(solution)/shard_map/pack/pallas_call | solution.py:361
  1.0 14.5 %all_to_all.10.recv_ref = f32[32,4,128]{2,1,0:T(4,128)S(1)} all-to-all(f32[32,4,128]{2,1,0:T(4,128)S(1)} %get-tuple-element.19), channel_id=1, replica_groups=mesh['vert'=8,'col'=4] {'vert','col'}, dimensions={0} | all-to-all | bytes 131072 | tf_op jit(solution)/shard_map/all_to_all | solution.py:376
  15.6 0.7 %shape.1 = (s16[32,8,128]{2,1,0:T(8,128)(2,1)S(1)}, f32[3,8,128]{2,1,0:T(8,128)S(1)}, f32[4,8,128]{2,1,0:T(8,128)S(1)}, bf16[128,128]{1,0:T(8,128)(2,1)S(1)}, f3...) custom-call(f32[32,4,128]{2,1,0:T(4,128)S(1)} %all_to_all.10.recv_ref, ...), custom_call_target="tpu_custom_call" | custom-call | tf_op jit(solution)/shard_map/shape/pallas_call | solution.py:377
  16.3 9.1 %all_to_all.11.recv_ref = s16[32,8,128]{2,1,0:T(8,128)(2,1)S(1)} all-to-all(s16[32,8,128]{2,1,0:T(8,128)(2,1)S(1)} %get-tuple-element.26), channel_id=1, replica_groups=mesh['vert'=8,'col'=4] {'vert','col'}, dimensions={0} | all-to-all | bytes 131072 | tf_op jit(solution)/shard_map/all_to_all | solution.py:402
  25.4 1.0 %pose.1 = bf16[3,2,656]{2,1,0:T(2,128)(2,1)} custom-call(s16[32,8,128]{2,1,0:T(8,128)(2,1)S(1)} %all_to_all.11.recv_ref, f32[3,8,128]{2,1,0:T(8,128)S(1)} %get-tuple-element.27.table_ref, f32[4,8,128]{2,1,0:T(8,128)S(1)} %get-tuple-element.28.diff_ref, bf16[128,128]{1,0:T(8,128)(2,1)S(1)} %get-tuple-element.29.above_ref, ...), custom_call_target="tpu_custom_call" | custom-call | tf_op jit(solution)/shard_map/pose/pallas_call | solution.py:403

commit v4 on v3

--- a/solution.py
+++ b/solution.py
@@ -66,6 +66,22 @@
     for copy in copies:
         copy.start()
     return copies
+
+
+def member(place, half):
+    return (place + half - 1) % half
+
+
+def halves(spans, groups, root):
+    half = groups // 2
+    return [
+        [
+            (root + span) % spans * groups + side * half + member(place, half)
+            for span in range(spans)
+            for place in range(half)
+        ]
+        for side in range(2)
+    ]
 
 
 def coder(verts, block):
@@ -84,10 +100,11 @@
         [(coeffs_hbm, coeffs_s), (index_hbm, index_s), (raw_hbm, raw_s), *zip(sources, targets)], sems
     )
     own_chars, comps = coeffs_s.shape
+    half = groups // 2
     block = comps // groups
     slots, verts = index_s.shape
-    per_group = slots // groups
-    column = lax.axis_index("col")
+    per_group = slots // half
+    column = lax.rem(lax.axis_index("col"), half)
     row_s[...] = jnp.zeros_like(row_s)
     for copy in copies[:3]:
         copy.wait()
@@ -96,24 +113,30 @@
     raw = raw_s[...]
     for which in range(per_group):
         sel = lax.broadcasted_iota(jnp.int32, index.shape, 0) == column * per_group + which
-        at = own_chars + 2 * which
+        at = 2 * own_chars + 2 * which
         for more, value in enumerate((index, raw)):
             value = jnp.sum(jnp.where(sel, value, 0.0), axis=0, keepdims=True)
-            for group in range(groups):
-                row_s[group, at + more : at + more + 1, 0:verts] = value
-    for group in range(groups):
-        row_s[group, 0:own_chars, 0:block] = wide[:, group * block : (group + 1) * block]
-    for group in range(groups):
-        value = row_s[group]
+            for place in range(half):
+                row_s[place, at + more : at + more + 1, 0:verts] = value
+    for place in range(half):
+        for side in range(2):
+            low = (side * half + member(place, half)) * block
+            row_s[place, side * own_chars : (side + 1) * own_chars, 0:block] = wide[:, low : low + block]
+    for place in range(half):
+        value = row_s[place]
         for span in range(spans):
-            out_ref[span * groups + group] = value
+            out_ref[span * half + place] = value
     for copy in copies[3:]:
         copy.wait()
 
 
 def shape_kernel(
-    groups,
-    recv_ref,
+    half,
+    slots,
+    root,
+    turn,
+    flat_ref,
+    other_ref,
     basis_ref,
     template_ref,
     regressor_ref,
@@ -137,9 +160,9 @@
 ):
     _, verts, block = basis_ref.shape
     own_chars, _, joints = quat_ref.shape
-    count = recv_ref.shape[0]
-    spans = count // groups
-    slots = index_ref.shape[0]
+    height = 2 * own_chars + 2 * slots // half
+    count = flat_ref.shape[0] // height
+    spans = count // half
     start, first, rest, step = layout(verts, joints)
     lane = lax.broadcasted_iota(jnp.int32, (SUBS, LANES), 1)
     sub = lax.broadcasted_iota(jnp.int32, (SUBS, LANES), 0)
@@ -158,24 +181,42 @@
             value = jnp.where(row == n, values[n], value)
         return value
 
+    side = lax.div(lax.axis_index("col"), half)
     pad_s[...] = jnp.zeros_like(pad_s)
     for coord in range(3):
-        pad_s[coord, 0:verts, 0:block] = basis_ref[coord]
+        pad_s[side, coord, 0:verts, 0:block] = basis_ref[coord]
+        pad_s[1 - side, coord, 0:verts, 0:block] = other_ref[coord]
     temp_s[...] = jnp.zeros_like(temp_s)
-    temp_s[0:3, 0:verts] = template_ref[...] * (1.0 / groups)
+    temp_s[0:3, 0:verts] = template_ref[...] * (1.0 / half)
     reg_s[...] = jnp.zeros_like(reg_s)
     reg_s[start:LANES, 0:verts] = regressor_ref[0:first, :]
     reg_s[LANES : LANES + rest, 0:verts] = regressor_ref[first:joints, :]
     reg_high, reg_low = split_two(reg_s[...])
     reg_all = jnp.concatenate([reg_high, reg_low, reg_high], axis=1)
-    chunk = min(32, count)
+    chunk = min(16, count)
     total = own_chars * chunk
-    unit, rate = coder(verts, block)
+    unit, rate = coder(verts, 2 * block)
 
     def do_chunk(number):
-        at = pl.ds(number * chunk, chunk)
-        coeffs = jnp.concatenate([recv_ref[at, char, :] for char in range(own_chars)], axis=0).astype(BF16)
-        shapes = [dot_across(coeffs, pad_s[coord]) + temp_s[coord : coord + 1, :] for coord in range(3)]
+        at = number * chunk * height
+        coeffs = jnp.concatenate(
+            [
+                jnp.concatenate(
+                    [
+                        flat_ref[pl.ds(at + part * own_chars + char, chunk, stride=height), :]
+                        for char in range(own_chars)
+                    ],
+                    axis=0,
+                )
+                for part in range(2)
+            ],
+            axis=1,
+        ).astype(BF16)
+        shapes = [
+            dot_across(coeffs, jnp.concatenate([pad_s[0, coord], pad_s[1, coord]], axis=1))
+            + temp_s[coord : coord + 1, :]
+            for coord in range(3)
+        ]
         high, low = split_two(jnp.concatenate(shapes, axis=0))
         sums = dot_across(jnp.concatenate([high, high, low], axis=1), reg_all)
         last = sums[0:total, LANES:]
@@ -186,10 +227,13 @@
             code = jnp.log(1.0 + jnp.abs(value) * (1.0 / unit)) * (1.0 / rate)
             code = jnp.where(value < 0.0, -code, code)
             for char in range(own_chars):
-                sum_s[:, place * own_chars + char, :] = code[char * chunk : (char + 1) * chunk]
-        out_ref[at] = jnp.round(sum_s[...]).astype(jnp.int32).astype(jnp.int16)
+                sum_s[pl.ds(number * chunk, chunk), place * own_chars + char, :] = code[
+                    char * chunk : (char + 1) * chunk
+                ]
 
     each(count // chunk, 1, do_chunk)
+    for low, high, shift in ((0, count - turn, turn), (count - turn, count, turn - count)):
+        out_ref[low + shift : high + shift] = jnp.round(sum_s[low:high]).astype(jnp.int32).astype(jnp.int16)
 
     quat_s[...] = jnp.zeros_like(quat_s)
     quat_s[:, 0:1, :] = jnp.ones_like(quat_s[:, 0:1, :])
@@ -247,22 +291,40 @@
             moved = jnp.where(sub == a * own_chars + char, move_ref[char : char + 1, a : a + 1], moved)
     shift_ref[...] = moved
 
+    per_group = slots // half
+    for base in range(0, spans, SUBS):
+        many = min(SUBS, spans - base)
+        rows = [None] * (2 * slots)
+        for place in range(half):
+            for more in range(2 * per_group):
+                at = (base * half + place) * height + 2 * own_chars + more
+                rows[2 * per_group * member(place, half) + more] = flat_ref[
+                    pl.ds(at, many, stride=half * height), :
+                ]
+        scale = 1.0 / sum_of(rows[1::2])
+        rows[1::2] = [value * scale for value in rows[1::2]]
+        for n, value in enumerate(rows):
+            skin_s[pl.ds(base * 2 * slots + n, many, stride=2 * slots), :] = value
+    tiles = index_ref.shape[1] // LANES
+    values = [None] * tiles
+    wide_lane = lax.broadcasted_iota(jnp.int32, (2 * slots, LANES), 1)
     for span in range(spans):
-        for group in range(groups):
-            value = recv_ref[span * groups + group, own_chars:, :]
-            rows = value.shape[0]
-            skin_s[group * rows : (group + 1) * rows, span * verts : (span + 1) * verts] = value[:, :verts]
-    norm = sum_of([skin_s[2 * n + 1 : 2 * n + 2, :] for n in range(slots)])
-    scale = 1.0 / norm
-    index_ref[...] = jnp.zeros_like(index_ref)
-    share_ref[...] = jnp.zeros_like(share_ref)
-    for n in range(slots):
-        index_ref[n : n + 1, : spans * verts] = skin_s[2 * n : 2 * n + 1, :].astype(jnp.int32)
-        share_ref[n : n + 1, : spans * verts] = skin_s[2 * n + 1 : 2 * n + 2, :] * scale
+        at = (span - root) % spans * 2 * slots
+        value = skin_s[at : at + 2 * slots, :]
+        low = span * verts
+        value = pltpu.roll(value, low % LANES, 1) if low % LANES else value
+        for tile in range(low // LANES, (low + verts - 1) // LANES + 1):
+            begin = low - tile * LANES
+            values[tile] = value if begin <= 0 else jnp.where(wide_lane >= begin, value, values[tile])
+    for tile in range(tiles):
+        at = slice(tile * LANES, (tile + 1) * LANES)
+        index_ref[:, at] = values[tile].astype(jnp.int32)
+        share_ref[:, at] = values[tile]
 
 
 def pose_kernel(
-    groups,
+    half,
+    root,
     own_chars,
     verts,
     block,
@@ -276,15 +338,15 @@
     out_ref,
     total_s,
 ):
-    spans = recv_ref.shape[0] // groups
-    slots = index_ref.shape[0]
+    spans = recv_ref.shape[0] // half
+    slots = index_ref.shape[0] // 2
     width = out_ref.shape[2]
     tiles = -(-width // LANES)
     lane = lax.broadcasted_iota(jnp.int32, (SUBS, LANES), 1)
     sub = lax.broadcasted_iota(jnp.int32, (SUBS, LANES), 0)
     row = sub // own_chars
     char_of = sub % own_chars
-    unit, rate = coder(verts, block)
+    unit, rate = coder(verts, 2 * block)
 
     def decode(number):
         code = recv_ref[number].astype(jnp.int32).astype(F32)
@@ -294,7 +356,8 @@
     total = None
     shapes = [None] * tiles
     for span in range(spans):
-        value = sum_of([decode(span * groups + group) for group in range(groups)])
+        at = (span - root) % spans * half
+        value = sum_of([decode(at + place) for place in range(half)])
         total = value if total is None else total + value
         low = span * verts
         turned = pltpu.roll(value, low % LANES, 1) if low % LANES else value
@@ -318,8 +381,8 @@
     for tile in range(tiles):
         end = min(width, (tile + 1) * LANES)
         at = slice(tile * LANES, (tile + 1) * LANES)
-        index = [jnp.broadcast_to(index_ref[n : n + 1, at], (SUBS, LANES)) for n in range(slots)]
-        share = [share_ref[n : n + 1, at] for n in range(slots)]
+        index = [jnp.broadcast_to(index_ref[2 * n : 2 * n + 1, at], (SUBS, LANES)) for n in range(slots)]
+        share = [share_ref[2 * n + 1 : 2 * n + 2, at] for n in range(slots)]
 
         def blend(table):
             return sum_of([share[n] * pick(table, index[n]) for n in range(slots)])
@@ -344,9 +407,12 @@
     own_chars, comps = coeffs.shape
     verts, slots = skin_index.shape
     joints = regressor.shape[0]
-    devices = spans * groups
+    half = groups // 2
+    members = spans * half
     block = comps // groups
-    rows = own_chars + 2 * slots // groups
+    rows = 2 * own_chars + 2 * slots // half
+    roots = (spans // 2, spans // 4)
+    turn = (roots[0] - roots[1]) % spans * half
     padded = round_up(spans * verts, LANES)
     whole = jax.ShapeDtypeStruct
     room = pltpu.CompilerParams(vmem_limit_bytes=16 * 2**20)
@@ -358,50 +424,57 @@
         translation,
         parents.reshape(1, joints),
     ]
+    other = lax.ppermute(local[0], "col", [(n, (n + half) % groups) for n in range(groups)])
+
+    def exchange(value, root):
+        return lax.all_to_all(
+            value, ("vert", "col"), 0, 0, tiled=True, axis_index_groups=halves(spans, groups, root)
+        )
+
     message, *local = pl.pallas_call(
         functools.partial(pack_kernel, groups, spans),
-        out_shape=[whole((devices, rows, LANES), F32)] + [whole(value.shape, value.dtype) for value in local],
+        out_shape=[whole((members, rows, LANES), F32)] + [whole(value.shape, value.dtype) for value in local],
         in_specs=[HBM] * (3 + len(local)),
         out_specs=[VMEM] * (1 + len(local)),
         scratch_shapes=[
             pltpu.VMEM((own_chars, comps), BF16),
             pltpu.VMEM((slots, verts), jnp.int32),
             pltpu.VMEM((slots, verts), F32),
-            pltpu.VMEM((groups, rows, LANES), F32),
+            pltpu.VMEM((half, rows, LANES), F32),
             pltpu.SemaphoreType.DMA((3 + len(local),)),
         ],
         compiler_params=room,
         name="pack",
     )(*in_hbm(coeffs, skin_index.T, skin_raw.T, *local))
-    received = lax.all_to_all(message, ("vert", "col"), 0, 0, tiled=True)
+    received = exchange(message, roots[0])
     partials, *local = pl.pallas_call(
-        functools.partial(shape_kernel, groups),
+        functools.partial(shape_kernel, half, slots, roots[0], turn),
         out_shape=[
-            whole((devices, 4 * own_chars, LANES), jnp.int16),
+            whole((members, 4 * own_chars, LANES), jnp.int16),
             whole((3, SUBS, LANES), F32),
             whole((4, SUBS, LANES), F32),
             whole((LANES, LANES), BF16),
             whole((SUBS, LANES), F32),
-            whole((slots, padded), jnp.int32),
-            whole((slots, padded), F32),
+            whole((2 * slots, padded), jnp.int32),
+            whole((2 * slots, padded), F32),
         ],
-        in_specs=[VMEM] * 7,
+        in_specs=[VMEM] * 8,
         out_specs=[VMEM] * 7,
         scratch_shapes=[
-            pltpu.VMEM((3, LANES, LANES), BF16),
+            pltpu.VMEM((2, 3, LANES, LANES), BF16),
             pltpu.VMEM((SUBS, LANES), F32),
             pltpu.VMEM((2 * LANES, LANES), F32),
             pltpu.VMEM((own_chars, 4, LANES), F32),
             pltpu.VMEM((SUBS, LANES), jnp.int32),
-            pltpu.VMEM((2 * slots, spans * verts), F32),
-            pltpu.VMEM((min(32, devices), 4 * own_chars, LANES), F32),
+            pltpu.VMEM((spans * 2 * slots, LANES), F32),
+            pltpu.VMEM((members, 4 * own_chars, LANES), F32),
         ],
         compiler_params=room,
         name="shape",
-    )(received, *local)
-    received = lax.all_to_all(partials, ("vert", "col"), 0, 0, tiled=True)
+    )(received.reshape(members * rows, LANES), other, *local)
+    received = exchange(partials, roots[1])
     posed = pl.pallas_call(
-        functools.partial(pose_kernel, groups, own_chars, verts, block),
+        functools.partial(pose_kernel, half, roots[1], own_chars, verts, block),
         out_shape=whole((3, own_chars, spans * verts), BF16),
         in_specs=[VMEM] * 7,
         out_specs=VMEM,

time: 26.5 us -> 24.7 us (0.932)
  blocking collectives: 23.6 us -> 8.73 us
  starting transfers between devices: 0 us -> 9.31 us
  waiting for transfers between devices: 0 us -> 3.06 us
  Pallas kernels: 2.7 us -> 3.28 us
    all_to_all x2 -> x1, blocking collectives: 23.6 us -> 8.73 us  [exchange(): lax.all_to_all(value, ('vert', 'col'), 0, 0, tiled=True, axis_index_group...]
    all_to_all x0 -> x1, starting transfers between devices: none -> 7.75 us  [exchange(): lax.all_to_all(value, ('vert', 'col'), 0, 0, tiled=True, axis_index_group...]
    ppermute x0 -> x1, waiting for transfers between devices: none -> 2.8 us  [body(): lax.ppermute(local[0], 'col', [(n, (n + half) % groups) for n in range(gr...]
    ppermute x0 -> x1, starting transfers between devices: none -> 1.56 us  [body(): lax.ppermute(local[0], 'col', [(n, (n + half) % groups) for n in range(gr...]
    pallas_call x1, Pallas kernels: 1.02 us -> 1.63 us  [body(): pl.pallas_call(functools.partial(pack_kernel, groups, spans), out_shape=[...]
    all_to_all x0 -> x1, waiting for transfers between devices: none -> 0.27 us  [exchange(): lax.all_to_all(value, ('vert', 'col'), 0, 0, tiled=True, axis_index_group...]
  transfers between devices with their start and end apart: 0 -> 2, of which waited for: 0 -> 2; matrix products, arithmetic and copies ran while one was open for 0% -> 0% of each run, Pallas kernels for 0% -> 0%
where the time goes in v4:
time: 24.7 us; the launch traced here: 24.4 us
  starting transfers between devices  9.31 us (38%)
  blocking collectives  8.73 us (35%)
  Pallas kernels  3.28 us (13%)
  waiting for transfers between devices  3.06 us (12%)
    all_to_all x1, blocking collectives, exchange(): lax.all_to_all(value, ('vert', 'col'), 0, 0, tiled=True, axis_index_group...  8.73 us
    all_to_all x1, starting transfers between devices, exchange(): lax.all_to_all(value, ('vert', 'col'), 0, 0, tiled=True, axis_index_group...  7.75 us
    ppermute x1, waiting for transfers between devices, body(): lax.ppermute(local[0], 'col', [(n, (n + half) % groups) for n in range(gr...  2.8 us
    pallas_call x1, Pallas kernels, body(): pl.pallas_call(functools.partial(pack_kernel, groups, spans), out_shape=[...  1.63 us
    ppermute x1, starting transfers between devices, body(): lax.ppermute(local[0], 'col', [(n, (n + half) % groups) for n in range(gr...  1.56 us
    pallas_call x1, Pallas kernels, body(): pl.pallas_call(functools.partial(pose_kernel, half, roots[1], own_chars,...  0.96 us
    pallas_call x1, Pallas kernels, body(): pl.pallas_call(functools.partial(shape_kernel, half, slots, roots[0], tur...  0.69 us
  transfers between devices with their start and end apart: 2, of which 2 were waited for; matrix products, arithmetic and copies ran while one was open for 0% of the time, Pallas kernels for 0%

profile of v4, /device:TPU:0, one launch (start us, length us, event | category | flops | bytes accessed | tf_op | source)
XLA Modules:
  0.0 24.4 jit_solution(1272214313235191255)
XLA Ops:
  0.0 1.6 %pack.1 = (f32[16,8,128]{2,1,0:T(8,128)}, bf16[3,82,100]{2,1,0:T(8,128)(2,1)S(1)}, f32[3,82]{1,0:T(4,128)S(1)}, f32[55,82]{1,0:T(8,128)S(1)}, f32[2,4,55]{2,1,0:...) custom-call(bf16[2,400]{1,0:T(2,128)(2,1)} %coeffs_hbm.1, s32[4,82]{1,0:T(4,128)} %bitcast.9, f32[4,82]{1,0:T(4,128)} %bitcast.10, ...), custom_call_target="tpu_custom_call" | custom-call | tf_op jit(solution)/shard_map/pack/pallas_call | solution.py:434
  1.6 0.0 copy-start
  1.7 7.8 %all-to-all-start = ((f32[16,8,128]{2,1,0:T(8,128)}), f32[16,8,128]{2,1,0:T(8,128)S(1)}, u32[]{:S(2)}, u32[]{:S(2)}) async-start(f32[16,8,128]{2,1,0:T(8,128)} %get-tuple-element.19), calls=%async_computation | async-start | bytes 131072 | tf_op jit(solution)/shard_map/all_to_all | solution.py:430
  9.4 0.0 copy-done
  9.4 1.6 %collective-permute-start = (bf16[3,82,100]{2,1,0:T(8,128)(2,1)S(1)}, bf16[3,82,100]{2,1,0:T(8,128)(2,1)S(1)}, u32[]{:S(2)}, u32[]{:S(2)}) collective-permute-start(bf16[3,82,100]{2,1,0:T(8,128)(2,1)S(1)} %bitcast.8), channel_id=1, source_target_pairs={{0,2},{1,3},{2,0},{3,1},{4,6},{5,7},{6,4},{7,5},{8,10},{9,11},{10,... | collective-permute-start | bytes 147608 | tf_op jit(solution)/shard_map/ppermute | solution.py:427
  11.0 2.8 %collective-permute-done.other_ref = bf16[3,82,100]{2,1,0:T(8,128)(2,1)S(1)} collective-permute-done((bf16[3,82,100]{2,1,0:T(8,128)(2,1)S(1)}, bf16[3,82,100]{2,1,0:T(8,128)(2,1)S(1)}, u32[]{:S(2)}, u32[]{:S(2)}) %collective-permute-start) | collective-permute-done | bytes 49232 | tf_op jit(solution)/shard_map/ppermute | solution.py:427
  13.8 0.3 %all-to-all-done = f32[16,8,128]{2,1,0:T(8,128)S(1)} async-done(((f32[16,8,128]{2,1,0:T(8,128)}), f32[16,8,128]{2,1,0:T(8,128)S(1)}, u32[]{:S(2)}, u32[]{:S(2)}) %all-to-all-start) | async-done | bytes 65568 | tf_op jit(solution)/shard_map/all_to_all | solution.py:430
  14.0 0.7 %shape.1 = (s16[16,8,128]{2,1,0:T(8,128)(2,1)S(1)}, f32[3,8,128]{2,1,0:T(8,128)S(1)}, f32[4,8,128]{2,1,0:T(8,128)S(1)}, bf16[128,128]{1,0:T(8,128)(2,1)S(1)}, f3...) custom-call(f32[128,128]{1,0:T(8,128)S(1)} %bitcast.6, ...), custom_call_target="tpu_custom_call" | custom-call | tf_op jit(solution)/shard_map/shape/pallas_call | solution.py:450
  14.7 8.7 %all_to_all.10.recv_ref = s16[16,8,128]{2,1,0:T(8,128)(2,1)S(1)} all-to-all(s16[16,8,128]{2,1,0:T(8,128)(2,1)S(1)} %get-tuple-element.26), channel_id=1, replica_groups={{9,8,13,12,17,16,21,20,25,24,29,28,1,0,5,4},{11,10,15,14,19,18,23,22,27..., dimensions={0} | all-to-all | bytes 65536 | tf_op jit(solution)/shard_map/all_to_all | solution.py:430
  23.5 1.0 %pose.1 = bf16[3,2,656]{2,1,0:T(2,128)(2,1)} custom-call(s16[16,8,128]{2,1,0:T(8,128)(2,1)S(1)} %all_to_all.10.recv_ref, f32[3,8,128]{2,1,0:T(8,128)S(1)} %get-tuple-element.27.table_ref, f32[4,8,128]{2,1,0:T(8,128)S(1)} %get-tuple-element.28.diff_ref, bf16[128,128]{1,0:T(8,128)(2,1)S(1)} %get-tuple-element.29.above_ref, ...), custom_call_target="tpu_custom_call" | custom-call | tf_op jit(solution)/shard_map/pose/pallas_call | solution.py:476
Async XLA Ops:
  1.6 7.8 %copy-start = (bf16[100,3,82]{0,2,1:T(8,128)(2,1)S(1)}, bf16[100,3,82]{0,2,1:T(8,128)(2,1)}, u32[]{:S(2)}) copy-start(bf16[100,3,82]{0,2,1:T(8,128)(2,1)} %param.10) | copy-start | bytes 147604
  1.7 12.4 %all-to-all-start = ((f32[16,8,128]{2,1,0:T(8,128)}), f32[16,8,128]{2,1,0:T(8,128)S(1)}, u32[]{:S(2)}, u32[]{:S(2)}) async-start(f32[16,8,128]{2,1,0:T(8,128)} %get-tuple-element.19), calls=%async_computation | async-start | bytes 131072 | tf_op jit(solution)/shard_map/all_to_all | solution.py:430
  9.4 4.4 %collective-permute-start = (bf16[3,82,100]{2,1,0:T(8,128)(2,1)S(1)}, bf16[3,82,100]{2,1,0:T(8,128)(2,1)S(1)}, u32[]{:S(2)}, u32[]{:S(2)}) collective-permute-start(bf16[3,82,100]{2,1,0:T(8,128)(2,1)S(1)} %bitcast.8), channel_id=1, source_target_pairs={{0,2},{1,3},{2,0},{3,1},{4,6},{5,7},{6,4},{7,5},{8,10},{9,11},{10,... | collective-permute-start | bytes 147608 | tf_op jit(solution)/shard_map/ppermute | solution.py:427

commit v5 on v4

--- a/solution.py
+++ b/solution.py
@@ -92,21 +92,17 @@
     return unit, rate
 
 
-def pack_kernel(groups, spans, coeffs_hbm, index_hbm, raw_hbm, *refs):
-    passed = (len(refs) - 6) // 2
-    sources, out_ref, targets = refs[:passed], refs[passed], refs[passed + 1 : 2 * passed + 1]
-    coeffs_s, index_s, raw_s, row_s, sems = refs[2 * passed + 1 :]
-    copies = fetch(
-        [(coeffs_hbm, coeffs_s), (index_hbm, index_s), (raw_hbm, raw_s), *zip(sources, targets)], sems
-    )
+def pack_kernel(groups, spans, coeffs_hbm, index_hbm, raw_hbm, out_ref, coeffs_s, index_s, raw_s, row_s, sems):
+    copies = fetch([(coeffs_hbm, coeffs_s), (index_hbm, index_s), (raw_hbm, raw_s)], sems)
     own_chars, comps = coeffs_s.shape
     half = groups // 2
     block = comps // groups
     slots, verts = index_s.shape
     per_group = slots // half
     column = lax.rem(lax.axis_index("col"), half)
+    side = lax.div(lax.axis_index("col"), half)
     row_s[...] = jnp.zeros_like(row_s)
-    for copy in copies[:3]:
+    for copy in copies:
         copy.wait()
     wide = coeffs_s[...].astype(F32)
     index = index_s[...].astype(F32)
@@ -119,50 +115,55 @@
             for place in range(half):
                 row_s[place, at + more : at + more + 1, 0:verts] = value
     for place in range(half):
-        for side in range(2):
-            low = (side * half + member(place, half)) * block
-            row_s[place, side * own_chars : (side + 1) * own_chars, 0:block] = wide[:, low : low + block]
+        low = [(part * half + member(place, half)) * block for part in range(2)]
+        low = [wide[:, at : at + block] for at in low]
+        row_s[place, 0:own_chars, 0:block] = jnp.where(side == 0, low[0], low[1])
+        row_s[place, own_chars : 2 * own_chars, 0:block] = jnp.where(side == 0, low[1], low[0])
     for place in range(half):
         value = row_s[place]
         for span in range(spans):
             out_ref[span * half + place] = value
-    for copy in copies[3:]:
-        copy.wait()
-
-
-def shape_kernel(
+
+
+def prep_kernel(
     half,
-    slots,
-    root,
-    turn,
-    flat_ref,
-    other_ref,
-    basis_ref,
-    template_ref,
-    regressor_ref,
-    quat_ref,
-    move_ref,
-    parents_ref,
-    out_ref,
+    basis_hbm,
+    template_hbm,
+    regressor_hbm,
+    quat_hbm,
+    move_hbm,
+    parents_hbm,
+    own_ref,
+    temp_ref,
+    reg_ref,
     table_ref,
     diff_ref,
     above_ref,
     shift_ref,
-    index_ref,
-    share_ref,
-    pad_s,
-    temp_s,
+    basis_s,
+    template_s,
+    regressor_s,
+    quat_raw,
+    move_s,
+    parents_s,
     reg_s,
     quat_s,
     parent_s,
-    skin_s,
-    sum_s,
+    sems,
 ):
-    _, verts, block = basis_ref.shape
-    own_chars, _, joints = quat_ref.shape
-    height = 2 * own_chars + 2 * slots // half
-    count = flat_ref.shape[0] // height
-    spans = count // half
+    copies = fetch(
+        [
+            (basis_hbm, basis_s),
+            (template_hbm, template_s),
+            (regressor_hbm, regressor_s),
+            (quat_hbm, quat_raw),
+            (move_hbm, move_s),
+            (parents_hbm, parents_s),
+        ],
+        sems,
+    )
+    _, verts, block = basis_s.shape
+    own_chars, _, joints = quat_raw.shape
     start, first, rest, step = layout(verts, joints)
     lane = lax.broadcasted_iota(jnp.int32, (SUBS, LANES), 1)
     sub = lax.broadcasted_iota(jnp.int32, (SUBS, LANES), 0)
@@ -181,63 +182,24 @@
             value = jnp.where(row == n, values[n], value)
         return value
 
-    side = lax.div(lax.axis_index("col"), half)
-    pad_s[...] = jnp.zeros_like(pad_s)
-    for coord in range(3):
-        pad_s[side, coord, 0:verts, 0:block] = basis_ref[coord]
-        pad_s[1 - side, coord, 0:verts, 0:block] = other_ref[coord]
-    temp_s[...] = jnp.zeros_like(temp_s)
-    temp_s[0:3, 0:verts] = template_ref[...] * (1.0 / half)
+    own_ref[...] = jnp.zeros_like(own_ref)
+    temp_ref[...] = jnp.zeros_like(temp_ref)
     reg_s[...] = jnp.zeros_like(reg_s)
-    reg_s[start:LANES, 0:verts] = regressor_ref[0:first, :]
-    reg_s[LANES : LANES + rest, 0:verts] = regressor_ref[first:joints, :]
-    reg_high, reg_low = split_two(reg_s[...])
-    reg_all = jnp.concatenate([reg_high, reg_low, reg_high], axis=1)
-    chunk = min(16, count)
-    total = own_chars * chunk
-    unit, rate = coder(verts, 2 * block)
-
-    def do_chunk(number):
-        at = number * chunk * height
-        coeffs = jnp.concatenate(
-            [
-                jnp.concatenate(
-                    [
-                        flat_ref[pl.ds(at + part * own_chars + char, chunk, stride=height), :]
-                        for char in range(own_chars)
-                    ],
-                    axis=0,
-                )
-                for part in range(2)
-            ],
-            axis=1,
-        ).astype(BF16)
-        shapes = [
-            dot_across(coeffs, jnp.concatenate([pad_s[0, coord], pad_s[1, coord]], axis=1))
-            + temp_s[coord : coord + 1, :]
-            for coord in range(3)
-        ]
-        high, low = split_two(jnp.concatenate(shapes, axis=0))
-        sums = dot_across(jnp.concatenate([high, high, low], axis=1), reg_all)
-        last = sums[0:total, LANES:]
-        for coord in range(1, 3):
-            last = last + pltpu.roll(sums[coord * total : (coord + 1) * total, LANES:], coord * step, 1)
-        rows = [shapes[coord] + sums[coord * total : (coord + 1) * total, :LANES] for coord in range(3)]
-        for place, value in enumerate(rows + [last]):
-            code = jnp.log(1.0 + jnp.abs(value) * (1.0 / unit)) * (1.0 / rate)
-            code = jnp.where(value < 0.0, -code, code)
-            for char in range(own_chars):
-                sum_s[pl.ds(number * chunk, chunk), place * own_chars + char, :] = code[
-                    char * chunk : (char + 1) * chunk
-                ]
-
-    each(count // chunk, 1, do_chunk)
-    for low, high, shift in ((0, count - turn, turn), (count - turn, count, turn - count)):
-        out_ref[low + shift : high + shift] = jnp.round(sum_s[low:high]).astype(jnp.int32).astype(jnp.int16)
-
     quat_s[...] = jnp.zeros_like(quat_s)
     quat_s[:, 0:1, :] = jnp.ones_like(quat_s[:, 0:1, :])
-    quat_s[:, :, 0:joints] = quat_ref[...]
+    parent_s[...] = jnp.zeros_like(parent_s)
+    for copy in copies:
+        copy.wait()
+    for coord in range(3):
+        own_ref[coord, 0:verts, 0:block] = basis_s[coord]
+    temp_ref[0:3, 0:verts] = template_s[...] * (1.0 / half)
+    reg_s[start:LANES, 0:verts] = regressor_s[0:first, :]
+    reg_s[LANES : LANES + rest, 0:verts] = regressor_s[first:joints, :]
+    high, low = split_two(reg_s[...])
+    for n, value in enumerate((high, low, high)):
+        reg_ref[:, n * LANES : (n + 1) * LANES] = value
+
+    quat_s[:, :, 0:joints] = quat_raw[...]
     w, x, y, z = [
         by_char([quat_s[char, comp : comp + 1, :] for char in range(own_chars)]) for comp in range(4)
     ]
@@ -247,8 +209,7 @@
         by_row([two * (x * y - w * z), 1.0 - two * (x * x + z * z), two * (y * z + w * x)]),
         by_row([two * (x * z + w * y), two * (y * z - w * x), 1.0 - two * (x * x + y * y)]),
     ]
-    parent_s[...] = jnp.zeros_like(parent_s)
-    parent_s[0:1, 0:joints] = parents_ref[...]
+    parent_s[0:1, 0:joints] = parents_s[...]
     parent = jnp.broadcast_to(parent_s[0:1, :], (SUBS, LANES))
     parent = jnp.where((lane >= joints) | (lane == 0), joints, parent)
 
@@ -288,8 +249,83 @@
     moved = none
     for char in range(own_chars):
         for a in range(3):
-            moved = jnp.where(sub == a * own_chars + char, move_ref[char : char + 1, a : a + 1], moved)
+            moved = jnp.where(sub == a * own_chars + char, move_s[char : char + 1, a : a + 1], moved)
     shift_ref[...] = moved
+
+
+def shape_kernel(
+    half,
+    own_chars,
+    verts,
+    slots,
+    joints,
+    root,
+    turn,
+    flat_ref,
+    other_ref,
+    own_ref,
+    temp_ref,
+    reg_ref,
+    out_ref,
+    index_ref,
+    share_ref,
+    pad_s,
+    skin_s,
+    sum_s,
+):
+    block = other_ref.shape[2]
+    height = 2 * own_chars + 2 * slots // half
+    count = flat_ref.shape[0] // height
+    spans = count // half
+    step = layout(verts, joints)[3]
+
+    pad_s[...] = jnp.zeros_like(pad_s)
+    for coord in range(3):
+        pad_s[coord, 0:verts, 0:block] = other_ref[coord]
+    chunk = min(16, count)
+    total = own_chars * chunk
+    unit, rate = coder(verts, 2 * block)
+
+    def do_chunk(number):
+        at = number * chunk * height
+        coeffs = jnp.concatenate(
+            [
+                jnp.concatenate(
+                    [
+                        flat_ref[pl.ds(at + part * own_chars + char, chunk, stride=height), :]
+                        for char in range(own_chars)
+                    ],
+                    axis=0,
+                )
+                for part in range(2)
+            ],
+            axis=1,
+        ).astype(BF16)
+        shapes = [
+            dot_across(coeffs, jnp.concatenate([own_ref[coord], pad_s[coord]], axis=1))
+            + temp_ref[coord : coord + 1, :]
+            for coord in range(3)
+        ]
+        high, low = split_two(jnp.concatenate(shapes, axis=0))
+        sums = dot_across(jnp.concatenate([high, high, low], axis=1), reg_ref[...])
+        last = sums[0:total, LANES:]
+        for coord in range(1, 3):
+            last = last + pltpu.roll(sums[coord * total : (coord + 1) * total, LANES:], coord * step, 1)
+        rows = [shapes[coord] + sums[coord * total : (coord + 1) * total, :LANES] for coord in range(3)]
+        for place, value in enumerate(rows + [last]):
+            code = jnp.log(1.0 + jnp.abs(value) * (1.0 / unit)) * (1.0 / rate)
+            code = jnp.where(value < 0.0, -code, code)
+            for char in range(own_chars):
+                sum_s[pl.ds(number * chunk, chunk), place * own_chars + char, :] = code[
+                    char * chunk : (char + 1) * chunk
+                ]
+
+    each(count // chunk, 1, do_chunk)
+    for low, high, shift in ((0, count - turn, turn), (count - turn, count, turn - count)):
+        if high > low:
+            out_ref[low + shift : high + shift] = (
+                jnp.round(sum_s[low:high]).astype(jnp.int32).astype(jnp.int16)
+            )
 
     per_group = slots // half
     for base in range(0, spans, SUBS):
@@ -416,62 +452,76 @@
     padded = round_up(spans * verts, LANES)
     whole = jax.ShapeDtypeStruct
     room = pltpu.CompilerParams(vmem_limit_bytes=16 * 2**20)
-    local = [
-        shape_basis.transpose(1, 2, 0),
-        template,
-        regressor,
-        quaternions,
-        translation,
-        parents.reshape(1, joints),
-    ]
-    other = lax.ppermute(local[0], "col", [(n, (n + half) % groups) for n in range(groups)])
+    basis = shape_basis.transpose(1, 2, 0)
+    other = lax.ppermute(basis, "col", [(n, (n + half) % groups) for n in range(groups)])
 
     def exchange(value, root):
         return lax.all_to_all(
             value, ("vert", "col"), 0, 0, tiled=True, axis_index_groups=halves(spans, groups, root)
         )
 
-    message, *local = pl.pallas_call(
+    message = pl.pallas_call(
         functools.partial(pack_kernel, groups, spans),
-        out_shape=[whole((members, rows, LANES), F32)] + [whole(value.shape, value.dtype) for value in local],
-        in_specs=[HBM] * (3 + len(local)),
-        out_specs=[VMEM] * (1 + len(local)),
+        out_shape=whole((members, rows, LANES), F32),
+        in_specs=[HBM] * 3,
+        out_specs=VMEM,
         scratch_shapes=[
             pltpu.VMEM((own_chars, comps), BF16),
             pltpu.VMEM((slots, verts), jnp.int32),
             pltpu.VMEM((slots, verts), F32),
             pltpu.VMEM((half, rows, LANES), F32),
-            pltpu.SemaphoreType.DMA((3 + len(local),)),
+            pltpu.SemaphoreType.DMA((3,)),
         ],
         compiler_params=room,
         name="pack",
-    )(*in_hbm(coeffs, skin_index.T, skin_raw.T, *local))
+    )(*in_hbm(coeffs, skin_index.T, skin_raw.T))
     received = exchange(message, roots[0])
-    partials, *local = pl.pallas_call(
-        functools.partial(shape_kernel, half, slots, roots[0], turn),
+    own, temp, reg, *local = pl.pallas_call(
+        functools.partial(prep_kernel, half),
         out_shape=[
-            whole((members, 4 * own_chars, LANES), jnp.int16),
+            whole((3, LANES, LANES), BF16),
+            whole((SUBS, LANES), F32),
+            whole((2 * LANES, 3 * LANES), BF16),
             whole((3, SUBS, LANES), F32),
             whole((4, SUBS, LANES), F32),
             whole((LANES, LANES), BF16),
             whole((SUBS, LANES), F32),
+        ],
+        in_specs=[HBM] * 6,
+        out_specs=[VMEM] * 7,
+        scratch_shapes=[
+            pltpu.VMEM((3, verts, block), BF16),
+            pltpu.VMEM((3, verts), F32),
+            pltpu.VMEM((joints, verts), F32),
+            pltpu.VMEM((own_chars, 4, joints), F32),
+            pltpu.VMEM((own_chars, 3), F32),
+            pltpu.VMEM((1, joints), jnp.int32),
+            pltpu.VMEM((2 * LANES, LANES), F32),
+            pltpu.VMEM((own_chars, 4, LANES), F32),
+            pltpu.VMEM((SUBS, LANES), jnp.int32),
+            pltpu.SemaphoreType.DMA((6,)),
+        ],
+        compiler_params=room,
+        cost_estimate=pl.CostEstimate(flops=10**7, bytes_accessed=10**6, transcendentals=0),
+        name="prep",
+    )(*in_hbm(basis, template, regressor, quaternions, translation, parents.reshape(1, joints)))
+    partials, *skin = pl.pallas_call(
+        functools.partial(shape_kernel, half, own_chars, verts, slots, joints, roots[0], turn),
+        out_shape=[
+            whole((members, 4 * own_chars, LANES), jnp.int16),
             whole((2 * slots, padded), jnp.int32),
             whole((2 * slots, padded), F32),
         ],
-        in_specs=[VMEM] * 8,
-        out_specs=[VMEM] * 7,
+        in_specs=[VMEM] * 5,
+        out_specs=[VMEM] * 3,
         scratch_shapes=[
-            pltpu.VMEM((2, 3, LANES, LANES), BF16),
-            pltpu.VMEM((SUBS, LANES), F32),
-            pltpu.VMEM((2 * LANES, LANES), F32),
-            pltpu.VMEM((own_chars, 4, LANES), F32),
-            pltpu.VMEM((SUBS, LANES), jnp.int32),
+            pltpu.VMEM((3, LANES, LANES), BF16),
             pltpu.VMEM((spans * 2 * slots, LANES), F32),
             pltpu.VMEM((members, 4 * own_chars, LANES), F32),
         ],
         compiler_params=room,
         name="shape",
-    )(received.reshape(members * rows, LANES), other, *local)
+    )(received.reshape(members * rows, LANES), other, own, temp, reg)
     received = exchange(partials, roots[1])
     posed = pl.pallas_call(
         functools.partial(pose_kernel, half, roots[1], own_chars, verts, block),
@@ -481,7 +531,7 @@
         scratch_shapes=[pltpu.VMEM((SUBS, LANES), F32)],
         compiler_params=room,
         name="pose",
-    )(received, *local)
+    )(received, *local, *skin)
     return posed.transpose(1, 0, 2)
 
 

time: 24.7 us -> 24.4 us (0.988)
  waiting for transfers between devices: 3.06 us -> 1.46 us
  Pallas kernels: 3.28 us -> 4.54 us
    ppermute x1, waiting for transfers between devices: 2.8 us -> 1.19 us  [body(): lax.ppermute(basis, 'col', [(n, (n + half) % groups) for n in range(group...]
    pallas_call x2 -> x3, Pallas kernels: 2.32 us -> 3.59 us  [the longest x1 1.6 us: body(): pl.pallas_call(functools.partial(prep_kernel, half), out_shape=[whole((3,...]
  transfers between devices with their start and end apart: 2 -> 2, of which waited for: 2 -> 2; matrix products, arithmetic and copies ran while one was open for 0% -> 0% of each run, Pallas kernels for 0% -> 7%
where the time goes in v5:
time: 24.4 us; the launch traced here: 24.1 us
  starting transfers between devices  9.31 us (38%)
  blocking collectives  8.73 us (36%)
  Pallas kernels  4.54 us (19%)
  waiting for transfers between devices  1.46 us (6%)
    all_to_all x1, blocking collectives, exchange(): lax.all_to_all(value, ('vert', 'col'), 0, 0, tiled=True, axis_index_group...  8.73 us
    all_to_all x1, starting transfers between devices, exchange(): lax.all_to_all(value, ('vert', 'col'), 0, 0, tiled=True, axis_index_group...  7.75 us
    pallas_call x1, Pallas kernels, body(): pl.pallas_call(functools.partial(prep_kernel, half), out_shape=[whole((3,...  1.6 us
    ppermute x1, starting transfers between devices, body(): lax.ppermute(basis, 'col', [(n, (n + half) % groups) for n in range(group...  1.56 us
    pallas_call x1, Pallas kernels, body(): pl.pallas_call(functools.partial(pack_kernel, groups, spans), out_shape=w...  1.51 us
    ppermute x1, waiting for transfers between devices, body(): lax.ppermute(basis, 'col', [(n, (n + half) % groups) for n in range(group...  1.19 us
    pallas_call x1, Pallas kernels, body(): pl.pallas_call(functools.partial(pose_kernel, half, roots[1], own_chars,...  0.96 us
  transfers between devices with their start and end apart: 2, of which 2 were waited for; matrix products, arithmetic and copies ran while one was open for 0% of the time, Pallas kernels for 7%

profile of v5, /device:TPU:0, one launch (start us, length us, event | category | flops | bytes accessed | tf_op | source)
XLA Modules:
  0.0 24.1 jit_solution(3053234869807440936)
XLA Ops:
  0.0 1.5 %pack.1 = f32[16,8,128]{2,1,0:T(8,128)} custom-call(bf16[2,400]{1,0:T(2,128)(2,1)} %coeffs_hbm.1, s32[4,82]{1,0:T(4,128)} %bitcast.9, f32[4,82]{1,0:T(4,128)} %bitcast.10), custom_call_target="tpu_custom_call" | custom-call | tf_op jit(solution)/shard_map/pack/pallas_call | solution.py:463
  1.5 0.0 copy-start
  1.5 7.8 %all-to-all-start = ((f32[16,8,128]{2,1,0:T(8,128)}), f32[16,8,128]{2,1,0:T(8,128)S(1)}, u32[]{:S(2)}, u32[]{:S(2)}) async-start(f32[16,8,128]{2,1,0:T(8,128)} %pack.1), calls=%async_computation | async-start | bytes 131072 | tf_op jit(solution)/shard_map/all_to_all | solution.py:459
  9.3 0.0 copy-done
  9.3 1.6 %collective-permute-start = (bf16[3,82,100]{2,1,0:T(8,128)(2,1)S(1)}, bf16[3,82,100]{2,1,0:T(8,128)(2,1)S(1)}, u32[]{:S(2)}, u32[]{:S(2)}) collective-permute-start(bf16[3,82,100]{2,1,0:T(8,128)(2,1)S(1)} %bitcast.8), channel_id=1, source_target_pairs={{0,2},{1,3},{2,0},{3,1},{4,6},{5,7},{6,4},{7,5},{8,10},{9,11},{10,... | collective-permute-start | bytes 147608 | tf_op jit(solution)/shard_map/ppermute | solution.py:456
  10.8 1.6 %prep.1 = (bf16[3,128,128]{2,1,0:T(8,128)(2,1)S(1)}, f32[8,128]{1,0:T(8,128)S(1)}, bf16[256,384]{1,0:T(8,128)(2,1)S(1)}, f32[3,8,128]{2,1,0:T(8,128)S(1)}, f32[4...) custom-call(bf16[3,82,100]{2,1,0:T(8,128)(2,1)} %bitcast.7, f32[3,82]{1,0:T(4,128)} %template_hbm.1, ...), custom_call_target="tpu_custom_call" | custom-call | flops 10000000 | bytes 1000000 | tf_op jit(solution)/shard_map/prep/pallas_call | solution.py:479
  12.4 1.2 %collective-permute-done.other_ref = bf16[3,82,100]{2,1,0:T(8,128)(2,1)S(1)} collective-permute-done((bf16[3,82,100]{2,1,0:T(8,128)(2,1)S(1)}, bf16[3,82,100]{2,1,0:T(8,128)(2,1)S(1)}, u32[]{:S(2)}, u32[]{:S(2)}) %collective-permute-start) | collective-permute-done | bytes 49232 | tf_op jit(solution)/shard_map/ppermute | solution.py:456
  13.6 0.3 %all-to-all-done = f32[16,8,128]{2,1,0:T(8,128)S(1)} async-done(((f32[16,8,128]{2,1,0:T(8,128)}), f32[16,8,128]{2,1,0:T(8,128)S(1)}, u32[]{:S(2)}, u32[]{:S(2)}) %all-to-all-start) | async-done | bytes 65568 | tf_op jit(solution)/shard_map/all_to_all | solution.py:459
  13.9 0.5 %shape.1 = (s16[16,8,128]{2,1,0:T(8,128)(2,1)S(1)}, s32[8,768]{1,0:T(8,128)S(1)}, f32[8,768]{1,0:T(8,128)S(1)}) custom-call(f32[128,128]{1,0:T(8,128)S(1)} %bitcast.6, bf16[3,82,100]{2,1,0:T(8,128)(2,1)S(1)} %collective-permute-done.other_ref, bf16[3,128,128]{2,1,0:T(8,128)(2,1)S(1)} %get-tuple-element.15.own_ref, f32[8,128]{1,0:T(8,128)S(1)} %get-tuple-element.16.temp_ref, ...), custom_call_target="tpu_custom_call" | custom-call | tf_op jit(solution)/shard_map/shape/pallas_call | solution.py:508
  14.4 8.7 %all_to_all.10.recv_ref = s16[16,8,128]{2,1,0:T(8,128)(2,1)S(1)} all-to-all(s16[16,8,128]{2,1,0:T(8,128)(2,1)S(1)} %get-tuple-element.18), channel_id=1, replica_groups={{9,8,13,12,17,16,21,20,25,24,29,28,1,0,5,4},{11,10,15,14,19,18,23,22,27..., dimensions={0} | all-to-all | bytes 65536 | tf_op jit(solution)/shard_map/all_to_all | solution.py:459
  23.1 1.0 %pose.1 = bf16[3,2,656]{2,1,0:T(2,128)(2,1)} custom-call(s16[16,8,128]{2,1,0:T(8,128)(2,1)S(1)} %all_to_all.10.recv_ref, f32[3,8,128]{2,1,0:T(8,128)S(1)} %get-tuple-element.19.table_ref, f32[4,8,128]{2,1,0:T(8,128)S(1)} %get-tuple-element.20.diff_ref, bf16[128,128]{1,0:T(8,128)(2,1)S(1)} %get-tuple-element.21.above_ref, ...), custom_call_target="tpu_custom_call" | custom-call | tf_op jit(solution)/shard_map/pose/pallas_call | solution.py:526
Async XLA Ops:
  1.5 7.8 %copy-start = (bf16[100,3,82]{0,2,1:T(8,128)(2,1)S(1)}, bf16[100,3,82]{0,2,1:T(8,128)(2,1)}, u32[]{:S(2)}) copy-start(bf16[100,3,82]{0,2,1:T(8,128)(2,1)} %param.10) | copy-start | bytes 147604
  1.5 12.4 %all-to-all-start = ((f32[16,8,128]{2,1,0:T(8,128)}), f32[16,8,128]{2,1,0:T(8,128)S(1)}, u32[]{:S(2)}, u32[]{:S(2)}) async-start(f32[16,8,128]{2,1,0:T(8,128)} %pack.1), calls=%async_computation | async-start | bytes 131072 | tf_op jit(solution)/shard_map/all_to_all | solution.py:459
  9.3 4.4 %collective-permute-start = (bf16[3,82,100]{2,1,0:T(8,128)(2,1)S(1)}, bf16[3,82,100]{2,1,0:T(8,128)(2,1)S(1)}, u32[]{:S(2)}, u32[]{:S(2)}) collective-permute-start(bf16[3,82,100]{2,1,0:T(8,128)(2,1)S(1)} %bitcast.8), channel_id=1, source_target_pairs={{0,2},{1,3},{2,0},{3,1},{4,6},{5,7},{6,4},{7,5},{8,10},{9,11},{10,... | collective-permute-start | bytes 147608 | tf_op jit(solution)/shard_map/ppermute | solution.py:456

commit v6 on v5

--- a/solution.py
+++ b/solution.py
@@ -72,14 +72,14 @@
     return (place + half - 1) % half
 
 
-def halves(spans, groups, root):
+def order_of(spans, root, stride):
+    return [(root + stride * n) % spans for n in range(spans)]
+
+
+def halves(groups, order):
     half = groups // 2
     return [
-        [
-            (root + span) % spans * groups + side * half + member(place, half)
-            for span in range(spans)
-            for place in range(half)
-        ]
+        [span * groups + side * half + member(place, half) for span in order for place in range(half)]
         for side in range(2)
     ]
 
@@ -259,16 +259,18 @@
     verts,
     slots,
     joints,
-    root,
-    turn,
+    order,
+    next_order,
     flat_ref,
     other_ref,
     own_ref,
     temp_ref,
     reg_ref,
+    table_ref,
     out_ref,
     index_ref,
     share_ref,
+    coef_ref,
     pad_s,
     skin_s,
     sum_s,
@@ -321,11 +323,11 @@
                 ]
 
     each(count // chunk, 1, do_chunk)
-    for low, high, shift in ((0, count - turn, turn), (count - turn, count, turn - count)):
-        if high > low:
-            out_ref[low + shift : high + shift] = (
-                jnp.round(sum_s[low:high]).astype(jnp.int32).astype(jnp.int16)
-            )
+    for n, span in enumerate(next_order):
+        at = order.index(span) * half
+        out_ref[n * half : (n + 1) * half] = (
+            jnp.round(sum_s[at : at + half]).astype(jnp.int32).astype(jnp.int16)
+        )
 
     per_group = slots // half
     for base in range(0, spans, SUBS):
@@ -345,7 +347,7 @@
     values = [None] * tiles
     wide_lane = lax.broadcasted_iota(jnp.int32, (2 * slots, LANES), 1)
     for span in range(spans):
-        at = (span - root) % spans * 2 * slots
+        at = order.index(span) * 2 * slots
         value = skin_s[at : at + 2 * slots, :]
         low = span * verts
         value = pltpu.roll(value, low % LANES, 1) if low % LANES else value
@@ -356,21 +358,29 @@
         at = slice(tile * LANES, (tile + 1) * LANES)
         index_ref[:, at] = values[tile].astype(jnp.int32)
         share_ref[:, at] = values[tile]
+        coef = [None] * 3
+        for n in range(slots):
+            wide = jnp.broadcast_to(values[tile][2 * n : 2 * n + 1, :], (SUBS, LANES)).astype(jnp.int32)
+            share = values[tile][2 * n + 1 : 2 * n + 2, :]
+            terms = [share * pick(table_ref[part], wide) for part in range(3)]
+            coef = terms if n == 0 else [coef[part] + terms[part] for part in range(3)]
+        for part in range(3):
+            coef_ref[part, :, at] = coef[part]
 
 
 def pose_kernel(
     half,
-    root,
+    order,
     own_chars,
     verts,
     block,
     recv_ref,
-    table_ref,
     diff_ref,
     above_ref,
     shift_ref,
     index_ref,
     share_ref,
+    coef_ref,
     out_ref,
     total_s,
 ):
@@ -392,7 +402,7 @@
     total = None
     shapes = [None] * tiles
     for span in range(spans):
-        at = (span - root) % spans * half
+        at = order.index(span) * half
         value = sum_of([decode(at + place) for place in range(half)])
         total = value if total is None else total + value
         low = span * verts
@@ -413,26 +423,21 @@
     high = lhs.astype(BF16).astype(F32)
     moved = dot(jnp.concatenate([high, lhs - high], axis=0).astype(BF16), above_ref[...])
     moved = (moved[:SUBS] + moved[SUBS:]) + shift_ref[...]
-    tables = [table_ref[turn] for turn in range(3)]
     for tile in range(tiles):
         end = min(width, (tile + 1) * LANES)
         at = slice(tile * LANES, (tile + 1) * LANES)
         index = [jnp.broadcast_to(index_ref[2 * n : 2 * n + 1, at], (SUBS, LANES)) for n in range(slots)]
         share = [share_ref[2 * n + 1 : 2 * n + 2, at] for n in range(slots)]
-
-        def blend(table):
-            return sum_of([share[n] * pick(table, index[n]) for n in range(slots)])
-
         shape = shapes[tile].astype(BF16).astype(F32)
         by_one = pltpu.roll(shape, own_chars, 0)
         by_two = pltpu.roll(shape, 2 * own_chars, 0)
         by_three = pltpu.roll(shape, 3 * own_chars, 0)
         turned = (
-            blend(tables[0]) * shape
-            + blend(tables[1]) * jnp.where(row < 2, by_three, by_two)
-            + blend(tables[2]) * jnp.where(row < 1, by_two, by_one)
+            coef_ref[0, :, at] * shape
+            + coef_ref[1, :, at] * jnp.where(row < 2, by_three, by_two)
+            + coef_ref[2, :, at] * jnp.where(row < 1, by_two, by_one)
         )
-        posed = turned + blend(moved)
+        posed = turned + sum_of([share[n] * pick(moved, index[n]) for n in range(slots)])
         for a in range(3):
             out_ref[a, :, tile * LANES : end] = posed[
                 a * own_chars : (a + 1) * own_chars, : end - tile * LANES
@@ -447,17 +452,16 @@
     members = spans * half
     block = comps // groups
     rows = 2 * own_chars + 2 * slots // half
-    roots = (spans // 2, spans // 4)
-    turn = (roots[0] - roots[1]) % spans * half
+    orders = (order_of(spans, spans // 2 - 1, 5), order_of(spans, spans // 2 + 1, 5))
     padded = round_up(spans * verts, LANES)
     whole = jax.ShapeDtypeStruct
     room = pltpu.CompilerParams(vmem_limit_bytes=16 * 2**20)
     basis = shape_basis.transpose(1, 2, 0)
     other = lax.ppermute(basis, "col", [(n, (n + half) % groups) for n in range(groups)])
 
-    def exchange(value, root):
+    def exchange(value, order):
         return lax.all_to_all(
-            value, ("vert", "col"), 0, 0, tiled=True, axis_index_groups=halves(spans, groups, root)
+            value, ("vert", "col"), 0, 0, tiled=True, axis_index_groups=halves(groups, order)
         )
 
     message = pl.pallas_call(
@@ -475,8 +479,8 @@
         compiler_params=room,
         name="pack",
     )(*in_hbm(coeffs, skin_index.T, skin_raw.T))
-    received = exchange(message, roots[0])
-    own, temp, reg, *local = pl.pallas_call(
+    received = exchange(message, orders[0])
+    own, temp, reg, table, *local = pl.pallas_call(
         functools.partial(prep_kernel, half),
         out_shape=[
             whole((3, LANES, LANES), BF16),
@@ -506,14 +510,15 @@
         name="prep",
     )(*in_hbm(basis, template, regressor, quaternions, translation, parents.reshape(1, joints)))
     partials, *skin = pl.pallas_call(
-        functools.partial(shape_kernel, half, own_chars, verts, slots, joints, roots[0], turn),
+        functools.partial(shape_kernel, half, own_chars, verts, slots, joints, *orders),
         out_shape=[
             whole((members, 4 * own_chars, LANES), jnp.int16),
             whole((2 * slots, padded), jnp.int32),
             whole((2 * slots, padded), F32),
+            whole((3, SUBS, padded), F32),
         ],
-        in_specs=[VMEM] * 5,
-        out_specs=[VMEM] * 3,
+        in_specs=[VMEM] * 6,
+        out_specs=[VMEM] * 4,
         scratch_shapes=[
             pltpu.VMEM((3, LANES, LANES), BF16),
             pltpu.VMEM((spans * 2 * slots, LANES), F32),
@@ -521,10 +526,10 @@
         ],
         compiler_params=room,
         name="shape",
-    )(received.reshape(members * rows, LANES), other, own, temp, reg)
-    received = exchange(partials, roots[1])
+    )(received.reshape(members * rows, LANES), other, own, temp, reg, table)
+    received = exchange(partials, orders[1])
     posed = pl.pallas_call(
-        functools.partial(pose_kernel, half, roots[1], own_chars, verts, block),
+        functools.partial(pose_kernel, half, orders[1], own_chars, verts, block),
         out_shape=whole((3, own_chars, spans * verts), BF16),
         in_specs=[VMEM] * 7,
         out_specs=VMEM,

time: 24.4 us -> 23.3 us (0.955)
  blocking collectives: 8.73 us -> 7.9 us
  waiting for transfers between devices: 1.46 us -> 1.19 us
    all_to_all x1, blocking collectives: 8.73 us -> 7.9 us  [exchange(): lax.all_to_all(value, ('vert', 'col'), 0, 0, tiled=True, axis_index_group...]
    all_to_all x1, waiting for transfers between devices: 0.27 us -> 0.01 us  [exchange(): lax.all_to_all(value, ('vert', 'col'), 0, 0, tiled=True, axis_index_group...]
  transfers between devices with their start and end apart: 2 -> 2, of which waited for: 2 -> 1; matrix products, arithmetic and copies ran while one was open for 0% -> 0% of each run, Pallas kernels for 7% -> 7%
where the time goes in v6:
time: 23.3 us; the launch traced here: 22.9 us
  starting transfers between devices  9.31 us (40%)
  blocking collectives  7.9 us (34%)
  Pallas kernels  4.51 us (19%)
  waiting for transfers between devices  1.19 us (5%)
    all_to_all x1, blocking collectives, exchange(): lax.all_to_all(value, ('vert', 'col'), 0, 0, tiled=True, axis_index_group...  7.9 us
    all_to_all x1, starting transfers between devices, exchange(): lax.all_to_all(value, ('vert', 'col'), 0, 0, tiled=True, axis_index_group...  7.75 us
    pallas_call x1, Pallas kernels, body(): pl.pallas_call(functools.partial(prep_kernel, half), out_shape=[whole((3,...  1.6 us
    ppermute x1, starting transfers between devices, body(): lax.ppermute(basis, 'col', [(n, (n + half) % groups) for n in range(group...  1.56 us
    pallas_call x1, Pallas kernels, body(): pl.pallas_call(functools.partial(pack_kernel, groups, spans), out_shape=w...  1.51 us
    ppermute x1, waiting for transfers between devices, body(): lax.ppermute(basis, 'col', [(n, (n + half) % groups) for n in range(group...  1.19 us
    pallas_call x1, Pallas kernels, body(): pl.pallas_call(functools.partial(pose_kernel, half, orders[1], own_chars,...  0.91 us
    pallas_call x1, Pallas kernels, body(): pl.pallas_call(functools.partial(shape_kernel, half, own_chars, verts, sl...  0.49 us
  transfers between devices with their start and end apart: 2, of which 1 were waited for; matrix products, arithmetic and copies ran while one was open for 0% of the time, Pallas kernels for 7%

profile of v6, /device:TPU:0, one launch (start us, length us, event | category | flops | bytes accessed | tf_op | source)
XLA Modules:
  0.0 22.9 jit_solution(5495797953748674001)
XLA Ops:
  0.0 1.5 %pack.1 = f32[16,8,128]{2,1,0:T(8,128)} custom-call(bf16[2,400]{1,0:T(2,128)(2,1)} %coeffs_hbm.1, s32[4,82]{1,0:T(4,128)} %bitcast.9, f32[4,82]{1,0:T(4,128)} %bitcast.10), custom_call_target="tpu_custom_call" | custom-call | tf_op jit(solution)/shard_map/pack/pallas_call | solution.py:467
  1.5 0.0 copy-start
  1.5 7.7 %all-to-all-start = ((f32[16,8,128]{2,1,0:T(8,128)}), f32[16,8,128]{2,1,0:T(8,128)S(1)}, u32[]{:S(2)}, u32[]{:S(2)}) async-start(f32[16,8,128]{2,1,0:T(8,128)} %pack.1), calls=%async_computation | async-start | bytes 131072 | tf_op jit(solution)/shard_map/all_to_all | solution.py:463
  9.3 0.0 copy-done
  9.3 1.6 %collective-permute-start = (bf16[3,82,100]{2,1,0:T(8,128)(2,1)S(1)}, bf16[3,82,100]{2,1,0:T(8,128)(2,1)S(1)}, u32[]{:S(2)}, u32[]{:S(2)}) collective-permute-start(bf16[3,82,100]{2,1,0:T(8,128)(2,1)S(1)} %bitcast.8), channel_id=1, source_target_pairs={{0,2},{1,3},{2,0},{3,1},{4,6},{5,7},{6,4},{7,5},{8,10},{9,11},{10,... | collective-permute-start | bytes 147608 | tf_op jit(solution)/shard_map/ppermute | solution.py:460
  10.8 1.6 %prep.1 = (bf16[3,128,128]{2,1,0:T(8,128)(2,1)S(1)}, f32[8,128]{1,0:T(8,128)S(1)}, bf16[256,384]{1,0:T(8,128)(2,1)S(1)}, f32[3,8,128]{2,1,0:T(8,128)S(1)}, f32[4...) custom-call(bf16[3,82,100]{2,1,0:T(8,128)(2,1)} %bitcast.7, f32[3,82]{1,0:T(4,128)} %template_hbm.1, ...), custom_call_target="tpu_custom_call" | custom-call | flops 10000000 | bytes 1000000 | tf_op jit(solution)/shard_map/prep/pallas_call | solution.py:483
  12.4 1.2 %collective-permute-done.other_ref = bf16[3,82,100]{2,1,0:T(8,128)(2,1)S(1)} collective-permute-done((bf16[3,82,100]{2,1,0:T(8,128)(2,1)S(1)}, bf16[3,82,100]{2,1,0:T(8,128)(2,1)S(1)}, u32[]{:S(2)}, u32[]{:S(2)}) %collective-permute-start) | collective-permute-done | bytes 49232 | tf_op jit(solution)/shard_map/ppermute | solution.py:460
  13.6 0.0 all-to-all-done
  13.6 0.5 %shape.1 = (s16[16,8,128]{2,1,0:T(8,128)(2,1)S(1)}, s32[8,768]{1,0:T(8,128)S(1)}, f32[8,768]{1,0:T(8,128)S(1)}, f32[3,8,768]{2,1,0:T(8,128)S(1)}) custom-call(f32[128,128]{1,0:T(8,128)S(1)} %bitcast.6, bf16[3,82,100]{2,1,0:T(8,128)(2,1)S(1)} %collective-permute-done.other_ref, bf16[3,128,128]{2,1,0:T(8,128)(2,1)S(1)} %get-tuple-element.16.own_ref, ...), custom_call_target="tpu_custom_call" | custom-call | tf_op jit(solution)/shard_map/shape/pallas_call | solution.py:512
  14.1 7.9 %all_to_all.10.recv_ref = s16[16,8,128]{2,1,0:T(8,128)(2,1)S(1)} all-to-all(s16[16,8,128]{2,1,0:T(8,128)(2,1)S(1)} %get-tuple-element.20), channel_id=1, replica_groups={{21,20,9,8,29,28,17,16,5,4,25,24,13,12,1,0},{23,22,11,10,31,30,19,18,7,..., dimensions={0} | all-to-all | bytes 65536 | tf_op jit(solution)/shard_map/all_to_all | solution.py:463
  22.0 0.9 %pose.1 = bf16[3,2,656]{2,1,0:T(2,128)(2,1)} custom-call(s16[16,8,128]{2,1,0:T(8,128)(2,1)S(1)} %all_to_all.10.recv_ref, f32[4,8,128]{2,1,0:T(8,128)S(1)} %get-tuple-element.21.diff_ref, bf16[128,128]{1,0:T(8,128)(2,1)S(1)} %get-tuple-element.22.above_ref, f32[8,128]{1,0:T(8,128)S(1)} %get-tuple-element.23.shift_ref, ...), custom_call_target="tpu_custom_call" | custom-call | tf_op jit(solution)/shard_map/pose/pallas_call | solution.py:531
Async XLA Ops:
  1.5 7.8 %copy-start = (bf16[100,3,82]{0,2,1:T(8,128)(2,1)S(1)}, bf16[100,3,82]{0,2,1:T(8,128)(2,1)}, u32[]{:S(2)}) copy-start(bf16[100,3,82]{0,2,1:T(8,128)(2,1)} %param.10) | copy-start | bytes 147604
  1.5 12.1 %all-to-all-start = ((f32[16,8,128]{2,1,0:T(8,128)}), f32[16,8,128]{2,1,0:T(8,128)S(1)}, u32[]{:S(2)}, u32[]{:S(2)}) async-start(f32[16,8,128]{2,1,0:T(8,128)} %pack.1), calls=%async_computation | async-start | bytes 131072 | tf_op jit(solution)/shard_map/all_to_all | solution.py:463
  9.3 4.4 %collective-permute-start = (bf16[3,82,100]{2,1,0:T(8,128)(2,1)S(1)}, bf16[3,82,100]{2,1,0:T(8,128)(2,1)S(1)}, u32[]{:S(2)}, u32[]{:S(2)}) collective-permute-start(bf16[3,82,100]{2,1,0:T(8,128)(2,1)S(1)} %bitcast.8), channel_id=1, source_target_pairs={{0,2},{1,3},{2,0},{3,1},{4,6},{5,7},{6,4},{7,5},{8,10},{9,11},{10,... | collective-permute-start | bytes 147608 | tf_op jit(solution)/shard_map/ppermute | solution.py:460

commit v7 on v6

--- a/solution.py
+++ b/solution.py
@@ -38,7 +38,10 @@
 
 
 def sum_of(values):
-    return functools.reduce(lambda p, q: p + q, values)
+    values = list(values)
+    while len(values) > 1:
+        values = [sum(values[n + 1 : n + 2], values[n]) for n in range(0, len(values), 2)]
+    return values[0]
 
 
 def dot(lhs, rhs):
@@ -194,7 +197,9 @@
         own_ref[coord, 0:verts, 0:block] = basis_s[coord]
     temp_ref[0:3, 0:verts] = template_s[...] * (1.0 / half)
     reg_s[start:LANES, 0:verts] = regressor_s[0:first, :]
-    reg_s[LANES : LANES + rest, 0:verts] = regressor_s[first:joints, :]
+    for coord in range(3):
+        at = LANES + coord * step
+        reg_s[at : at + rest, 0:verts] = regressor_s[first:joints, :]
     high, low = split_two(reg_s[...])
     for n, value in enumerate((high, low, high)):
         reg_ref[:, n * LANES : (n + 1) * LANES] = value
@@ -286,6 +291,7 @@
         pad_s[coord, 0:verts, 0:block] = other_ref[coord]
     chunk = min(16, count)
     total = own_chars * chunk
+    rows_lane = lax.broadcasted_iota(jnp.int32, (total, LANES), 1)
     unit, rate = coder(verts, 2 * block)
 
     def do_chunk(number):
@@ -310,9 +316,11 @@
         ]
         high, low = split_two(jnp.concatenate(shapes, axis=0))
         sums = dot_across(jnp.concatenate([high, high, low], axis=1), reg_ref[...])
-        last = sums[0:total, LANES:]
-        for coord in range(1, 3):
-            last = last + pltpu.roll(sums[coord * total : (coord + 1) * total, LANES:], coord * step, 1)
+        last = sums[2 * total : 3 * total, LANES:]
+        for coord in (1, 0):
+            last = jnp.where(
+                rows_lane < (coord + 1) * step, sums[coord * total : (coord + 1) * total, LANES:], last
+            )
         rows = [shapes[coord] + sums[coord * total : (coord + 1) * total, :LANES] for coord in range(3)]
         for place, value in enumerate(rows + [last]):
             code = jnp.log(1.0 + jnp.abs(value) * (1.0 / unit)) * (1.0 / rate)
@@ -399,19 +407,19 @@
         value = jnp.exp(jnp.abs(code) * rate) * unit - unit
         return jnp.where(code < 0.0, -value, value)
 
-    total = None
+    parts = []
     shapes = [None] * tiles
     for span in range(spans):
         at = order.index(span) * half
         value = sum_of([decode(at + place) for place in range(half)])
-        total = value if total is None else total + value
+        parts.append(value)
         low = span * verts
         turned = pltpu.roll(value, low % LANES, 1) if low % LANES else value
         for tile in range(low // LANES, (low + verts - 1) // LANES + 1):
             begin = low - tile * LANES
             shapes[tile] = turned if begin <= 0 else jnp.where(lane >= begin, turned, shapes[tile])
 
-    total_s[...] = total
+    total_s[...] = sum_of(parts)
     terms = []
     for coord in range(4):
         pair = jnp.broadcast_to(total_s[coord * own_chars : coord * own_chars + 1, :], (SUBS, LANES))

time: 23.3 us -> 23.2 us (level)
  no operation moved by 1% of the time
where the time goes in v7:
time: 23.2 us; the launch traced here: 22.9 us
  starting transfers between devices  9.31 us (40%)
  blocking collectives  7.9 us (34%)
  Pallas kernels  4.45 us (19%)
  waiting for transfers between devices  1.19 us (5%)
    all_to_all x1, blocking collectives, exchange(): lax.all_to_all(value, ('vert', 'col'), 0, 0, tiled=True, axis_index_group...  7.9 us
    all_to_all x1, starting transfers between devices, exchange(): lax.all_to_all(value, ('vert', 'col'), 0, 0, tiled=True, axis_index_group...  7.75 us
    pallas_call x1, Pallas kernels, body(): pl.pallas_call(functools.partial(prep_kernel, half), out_shape=[whole((3,...  1.6 us
    ppermute x1, starting transfers between devices, body(): lax.ppermute(basis, 'col', [(n, (n + half) % groups) for n in range(group...  1.56 us
    pallas_call x1, Pallas kernels, body(): pl.pallas_call(functools.partial(pack_kernel, groups, spans), out_shape=w...  1.51 us
    ppermute x1, waiting for transfers between devices, body(): lax.ppermute(basis, 'col', [(n, (n + half) % groups) for n in range(group...  1.19 us
    pallas_call x1, Pallas kernels, body(): pl.pallas_call(functools.partial(pose_kernel, half, orders[1], own_chars,...  0.91 us
  transfers between devices with their start and end apart: 2, of which 1 were waited for; matrix products, arithmetic and copies ran while one was open for 0% of the time, Pallas kernels for 7%

profile of v7, /device:TPU:0, one launch (start us, length us, event | category | flops | bytes accessed | tf_op | source)
XLA Modules:
  0.0 22.9 jit_solution(11318998758075507335)
XLA Ops:
  0.0 1.5 %pack.1 = f32[16,8,128]{2,1,0:T(8,128)} custom-call(bf16[2,400]{1,0:T(2,128)(2,1)} %coeffs_hbm.1, s32[4,82]{1,0:T(4,128)} %bitcast.9, f32[4,82]{1,0:T(4,128)} %bitcast.10), custom_call_target="tpu_custom_call" | custom-call | tf_op jit(solution)/shard_map/pack/pallas_call | solution.py:475
  1.5 0.0 copy-start
  1.5 7.7 %all-to-all-start = ((f32[16,8,128]{2,1,0:T(8,128)}), f32[16,8,128]{2,1,0:T(8,128)S(1)}, u32[]{:S(2)}, u32[]{:S(2)}) async-start(f32[16,8,128]{2,1,0:T(8,128)} %pack.1), calls=%async_computation | async-start | bytes 131072 | tf_op jit(solution)/shard_map/all_to_all | solution.py:471
  9.3 0.0 copy-done
  9.3 1.6 %collective-permute-start = (bf16[3,82,100]{2,1,0:T(8,128)(2,1)S(1)}, bf16[3,82,100]{2,1,0:T(8,128)(2,1)S(1)}, u32[]{:S(2)}, u32[]{:S(2)}) collective-permute-start(bf16[3,82,100]{2,1,0:T(8,128)(2,1)S(1)} %bitcast.8), channel_id=1, source_target_pairs={{0,2},{1,3},{2,0},{3,1},{4,6},{5,7},{6,4},{7,5},{8,10},{9,11},{10,... | collective-permute-start | bytes 147608 | tf_op jit(solution)/shard_map/ppermute | solution.py:468
  10.8 1.6 %prep.1 = (bf16[3,128,128]{2,1,0:T(8,128)(2,1)S(1)}, f32[8,128]{1,0:T(8,128)S(1)}, bf16[256,384]{1,0:T(8,128)(2,1)S(1)}, f32[3,8,128]{2,1,0:T(8,128)S(1)}, f32[4...) custom-call(bf16[3,82,100]{2,1,0:T(8,128)(2,1)} %bitcast.7, f32[3,82]{1,0:T(4,128)} %template_hbm.1, ...), custom_call_target="tpu_custom_call" | custom-call | flops 10000000 | bytes 1000000 | tf_op jit(solution)/shard_map/prep/pallas_call | solution.py:491
  12.4 1.2 %collective-permute-done.other_ref = bf16[3,82,100]{2,1,0:T(8,128)(2,1)S(1)} collective-permute-done((bf16[3,82,100]{2,1,0:T(8,128)(2,1)S(1)}, bf16[3,82,100]{2,1,0:T(8,128)(2,1)S(1)}, u32[]{:S(2)}, u32[]{:S(2)}) %collective-permute-start) | collective-permute-done | bytes 49232 | tf_op jit(solution)/shard_map/ppermute | solution.py:468
  13.6 0.0 all-to-all-done
  13.6 0.4 %shape.1 = (s16[16,8,128]{2,1,0:T(8,128)(2,1)S(1)}, s32[8,768]{1,0:T(8,128)S(1)}, f32[8,768]{1,0:T(8,128)S(1)}, f32[3,8,768]{2,1,0:T(8,128)S(1)}) custom-call(f32[128,128]{1,0:T(8,128)S(1)} %bitcast.6, bf16[3,82,100]{2,1,0:T(8,128)(2,1)S(1)} %collective-permute-done.other_ref, bf16[3,128,128]{2,1,0:T(8,128)(2,1)S(1)} %get-tuple-element.16.own_ref, ...), custom_call_target="tpu_custom_call" | custom-call | tf_op jit(solution)/shard_map/shape/pallas_call | solution.py:520
  14.1 7.9 %all_to_all.10.recv_ref = s16[16,8,128]{2,1,0:T(8,128)(2,1)S(1)} all-to-all(s16[16,8,128]{2,1,0:T(8,128)(2,1)S(1)} %get-tuple-element.20), channel_id=1, replica_groups={{21,20,9,8,29,28,17,16,5,4,25,24,13,12,1,0},{23,22,11,10,31,30,19,18,7,..., dimensions={0} | all-to-all | bytes 65536 | tf_op jit(solution)/shard_map/all_to_all | solution.py:471
  22.0 0.9 %pose.1 = bf16[3,2,656]{2,1,0:T(2,128)(2,1)} custom-call(s16[16,8,128]{2,1,0:T(8,128)(2,1)S(1)} %all_to_all.10.recv_ref, f32[4,8,128]{2,1,0:T(8,128)S(1)} %get-tuple-element.21.diff_ref, bf16[128,128]{1,0:T(8,128)(2,1)S(1)} %get-tuple-element.22.above_ref, f32[8,128]{1,0:T(8,128)S(1)} %get-tuple-element.23.shift_ref, ...), custom_call_target="tpu_custom_call" | custom-call | tf_op jit(solution)/shard_map/pose/pallas_call | solution.py:539
Async XLA Ops:
  1.5 7.8 %copy-start = (bf16[100,3,82]{0,2,1:T(8,128)(2,1)S(1)}, bf16[100,3,82]{0,2,1:T(8,128)(2,1)}, u32[]{:S(2)}) copy-start(bf16[100,3,82]{0,2,1:T(8,128)(2,1)} %param.10) | copy-start | bytes 147604
  1.5 12.1 %all-to-all-start = ((f32[16,8,128]{2,1,0:T(8,128)}), f32[16,8,128]{2,1,0:T(8,128)S(1)}, u32[]{:S(2)}, u32[]{:S(2)}) async-start(f32[16,8,128]{2,1,0:T(8,128)} %pack.1), calls=%async_computation | async-start | bytes 131072 | tf_op jit(solution)/shard_map/all_to_all | solution.py:471
  9.3 4.4 %collective-permute-start = (bf16[3,82,100]{2,1,0:T(8,128)(2,1)S(1)}, bf16[3,82,100]{2,1,0:T(8,128)(2,1)S(1)}, u32[]{:S(2)}, u32[]{:S(2)}) collective-permute-start(bf16[3,82,100]{2,1,0:T(8,128)(2,1)S(1)} %bitcast.8), channel_id=1, source_target_pairs={{0,2},{1,3},{2,0},{3,1},{4,6},{5,7},{6,4},{7,5},{8,10},{9,11},{10,... | collective-permute-start | bytes 147608 | tf_op jit(solution)/shard_map/ppermute | solution.py:468

commit v8 on v7

--- a/solution.py
+++ b/solution.py
@@ -91,7 +91,7 @@
     shape = block * 6.0 * 0.3125 + 6.0
     limit = max(shape, verts * 0.5 * shape)
     unit = 2.0**-16
-    rate = math.log1p(limit / unit) / 32766.0
+    rate = math.log2(1.0 + limit / unit) / 32766.0
     return unit, rate
 
 
@@ -101,6 +101,7 @@
     half = groups // 2
     block = comps // groups
     slots, verts = index_s.shape
+    spare = LANES - verts
     per_group = slots // half
     column = lax.rem(lax.axis_index("col"), half)
     side = lax.div(lax.axis_index("col"), half)
@@ -112,18 +113,22 @@
     raw = raw_s[...]
     for which in range(per_group):
         sel = lax.broadcasted_iota(jnp.int32, index.shape, 0) == column * per_group + which
+        value = [jnp.sum(jnp.where(sel, value, 0.0), axis=0, keepdims=True) for value in (index, raw)]
+        high = value[1].astype(BF16).astype(F32)
+        low = value[1] - high
         at = 2 * own_chars + 2 * which
-        for more, value in enumerate((index, raw)):
-            value = jnp.sum(jnp.where(sel, value, 0.0), axis=0, keepdims=True)
-            for place in range(half):
-                row_s[place, at + more : at + more + 1, 0:verts] = value
+        for place in range(half):
+            row_s[place, at : at + 1, 0:verts] = value[0]
+            row_s[place, at : at + 1, verts:LANES] = low[:, 0:spare]
+            row_s[place, at + 1 : at + 2, 0:verts] = high
+            row_s[place, at + 1 : at + 2, verts : 2 * verts - spare] = low[:, spare:]
     for place in range(half):
         low = [(part * half + member(place, half)) * block for part in range(2)]
         low = [wide[:, at : at + block] for at in low]
         row_s[place, 0:own_chars, 0:block] = jnp.where(side == 0, low[0], low[1])
         row_s[place, own_chars : 2 * own_chars, 0:block] = jnp.where(side == 0, low[1], low[0])
     for place in range(half):
-        value = row_s[place]
+        value = row_s[place].astype(BF16)
         for span in range(spans):
             out_ref[span * half + place] = value
 
@@ -266,7 +271,7 @@
     joints,
     order,
     next_order,
-    flat_ref,
+    recv_ref,
     other_ref,
     own_ref,
     temp_ref,
@@ -279,11 +284,14 @@
     pad_s,
     skin_s,
     sum_s,
+    flat_ref,
 ):
     block = other_ref.shape[2]
     height = 2 * own_chars + 2 * slots // half
-    count = flat_ref.shape[0] // height
+    count = recv_ref.shape[0]
     spans = count // half
+    for n in range(count):
+        flat_ref[n * height : (n + 1) * height, :] = recv_ref[n].astype(F32)
     step = layout(verts, joints)[3]
 
     pad_s[...] = jnp.zeros_like(pad_s)
@@ -323,7 +331,7 @@
             )
         rows = [shapes[coord] + sums[coord * total : (coord + 1) * total, :LANES] for coord in range(3)]
         for place, value in enumerate(rows + [last]):
-            code = jnp.log(1.0 + jnp.abs(value) * (1.0 / unit)) * (1.0 / rate)
+            code = jnp.log2(1.0 + jnp.abs(value) * (1.0 / unit)) * (1.0 / rate)
             code = jnp.where(value < 0.0, -code, code)
             for char in range(own_chars):
                 sum_s[pl.ds(number * chunk, chunk), place * own_chars + char, :] = code[
@@ -347,6 +355,11 @@
                 rows[2 * per_group * member(place, half) + more] = flat_ref[
                     pl.ds(at, many, stride=half * height), :
                 ]
+        spare = LANES - verts
+        near = lax.broadcasted_iota(jnp.int32, (many, LANES), 1) < spare
+        for n in range(0, 2 * slots, 2):
+            low = jnp.where(near, pltpu.roll(rows[n], spare, 1), pltpu.roll(rows[n + 1], 2 * spare, 1))
+            rows[n + 1] = rows[n + 1] + low
         scale = 1.0 / sum_of(rows[1::2])
         rows[1::2] = [value * scale for value in rows[1::2]]
         for n, value in enumerate(rows):
@@ -404,7 +417,7 @@
 
     def decode(number):
         code = recv_ref[number].astype(jnp.int32).astype(F32)
-        value = jnp.exp(jnp.abs(code) * rate) * unit - unit
+        value = jnp.exp2(jnp.abs(code) * rate) * unit - unit
         return jnp.where(code < 0.0, -value, value)
 
     parts = []
@@ -474,7 +487,7 @@
 
     message = pl.pallas_call(
         functools.partial(pack_kernel, groups, spans),
-        out_shape=whole((members, rows, LANES), F32),
+        out_shape=whole((members, rows, LANES), BF16),
         in_specs=[HBM] * 3,
         out_specs=VMEM,
         scratch_shapes=[
@@ -531,10 +544,11 @@
             pltpu.VMEM((3, LANES, LANES), BF16),
             pltpu.VMEM((spans * 2 * slots, LANES), F32),
             pltpu.VMEM((members, 4 * own_chars, LANES), F32),
+            pltpu.VMEM((members * rows, LANES), F32),
         ],
         compiler_params=room,
         name="shape",
-    )(received.reshape(members * rows, LANES), other, own, temp, reg, table)
+    )(received, other, own, temp, reg, table)
     received = exchange(partials, orders[1])
     posed = pl.pallas_call(
         functools.partial(pose_kernel, half, orders[1], own_chars, verts, block),

time: 23.2 us -> 23.1 us (level)
  no operation moved by 1% of the time
where the time goes in v8:
time: 23.1 us; the launch traced here: 22.8 us
  starting transfers between devices  9.17 us (40%)
  blocking collectives  7.9 us (34%)
  Pallas kernels  4.48 us (19%)
  waiting for transfers between devices  1.19 us (5%)
    all_to_all x1, blocking collectives, exchange(): lax.all_to_all(value, ('vert', 'col'), 0, 0, tiled=True, axis_index_group...  7.9 us
    all_to_all x1, starting transfers between devices, exchange(): lax.all_to_all(value, ('vert', 'col'), 0, 0, tiled=True, axis_index_group...  7.62 us
    pallas_call x1, Pallas kernels, body(): pl.pallas_call(functools.partial(prep_kernel, half), out_shape=[whole((3,...  1.6 us
    ppermute x1, starting transfers between devices, body(): lax.ppermute(basis, 'col', [(n, (n + half) % groups) for n in range(group...  1.56 us
    pallas_call x1, Pallas kernels, body(): pl.pallas_call(functools.partial(pack_kernel, groups, spans), out_shape=w...  1.53 us
    ppermute x1, waiting for transfers between devices, body(): lax.ppermute(basis, 'col', [(n, (n + half) % groups) for n in range(group...  1.19 us
    pallas_call x1, Pallas kernels, body(): pl.pallas_call(functools.partial(pose_kernel, half, orders[1], own_chars,...  0.91 us
  transfers between devices with their start and end apart: 2, of which 1 were waited for; matrix products, arithmetic and copies ran while one was open for 0% of the time, Pallas kernels for 7%

profile of v8, /device:TPU:0, one launch (start us, length us, event | category | flops | bytes accessed | tf_op | source)
XLA Modules:
  0.0 22.8 jit_solution(17156590615021802004)
XLA Ops:
  0.0 0.0 copy-start
  0.0 1.5 %pack.1 = bf16[16,8,128]{2,1,0:T(8,128)(2,1)} custom-call(bf16[2,400]{1,0:T(2,128)(2,1)} %coeffs_hbm.1, s32[4,82]{1,0:T(4,128)} %bitcast.7, f32[4,82]{1,0:T(4,128)} %bitcast.8), custom_call_target="tpu_custom_call" | custom-call | tf_op jit(solution)/shard_map/pack/pallas_call | solution.py:488
  1.5 7.6 %all-to-all-start = ((bf16[16,8,128]{2,1,0:T(8,128)(2,1)}), bf16[16,8,128]{2,1,0:T(8,128)(2,1)S(1)}, u32[]{:S(2)}, u32[]{:S(2)}) async-start(bf16[16,8,128]{2,1,0:T(8,128)(2,1)} %pack.1), calls=%async_computation | async-start | bytes 65536 | tf_op jit(solution)/shard_map/all_to_all | solution.py:484
  9.2 0.0 copy-done
  9.2 1.6 %collective-permute-start = (bf16[3,82,100]{2,1,0:T(8,128)(2,1)S(1)}, bf16[3,82,100]{2,1,0:T(8,128)(2,1)S(1)}, u32[]{:S(2)}, u32[]{:S(2)}) collective-permute-start(bf16[3,82,100]{2,1,0:T(8,128)(2,1)S(1)} %bitcast.6), channel_id=1, source_target_pairs={{0,2},{1,3},{2,0},{3,1},{4,6},{5,7},{6,4},{7,5},{8,10},{9,11},{10,... | collective-permute-start | bytes 147608 | tf_op jit(solution)/shard_map/ppermute | solution.py:481
  10.7 1.6 %prep.1 = (bf16[3,128,128]{2,1,0:T(8,128)(2,1)S(1)}, f32[8,128]{1,0:T(8,128)S(1)}, bf16[256,384]{1,0:T(8,128)(2,1)S(1)}, f32[3,8,128]{2,1,0:T(8,128)S(1)}, f32[4...) custom-call(bf16[3,82,100]{2,1,0:T(8,128)(2,1)} %bitcast.5, f32[3,82]{1,0:T(4,128)} %template_hbm.1, ...), custom_call_target="tpu_custom_call" | custom-call | flops 10000000 | bytes 1000000 | tf_op jit(solution)/shard_map/prep/pallas_call | solution.py:504
  12.3 1.2 %collective-permute-done.other_ref = bf16[3,82,100]{2,1,0:T(8,128)(2,1)S(1)} collective-permute-done((bf16[3,82,100]{2,1,0:T(8,128)(2,1)S(1)}, bf16[3,82,100]{2,1,0:T(8,128)(2,1)S(1)}, u32[]{:S(2)}, u32[]{:S(2)}) %collective-permute-start) | collective-permute-done | bytes 49232 | tf_op jit(solution)/shard_map/ppermute | solution.py:481
  13.5 0.0 all-to-all-done.recv_ref
  13.5 0.4 %shape.1 = (s16[16,8,128]{2,1,0:T(8,128)(2,1)S(1)}, s32[8,768]{1,0:T(8,128)S(1)}, f32[8,768]{1,0:T(8,128)S(1)}, f32[3,8,768]{2,1,0:T(8,128)S(1)}) custom-call(bf16[16,8,128]{2,1,0:T(8,128)(2,1)S(1)} %all-to-all-done.recv_ref, bf16[3,82,100]{2,1,0:T(8,128)(2,1)S(1)} %collective-permute-done.other_ref, bf16[3,128,128]{2,1,0:T(8,128)(2,1)S(1)} %get-tuple-element.16.own_ref, ...), custom_call_target="tpu_custom_call" | custom-call | tf_op jit(solution)/shard_map/shape/pallas_call | solution.py:533
  14.0 7.9 %all_to_all.10.recv_ref = s16[16,8,128]{2,1,0:T(8,128)(2,1)S(1)} all-to-all(s16[16,8,128]{2,1,0:T(8,128)(2,1)S(1)} %get-tuple-element.20), channel_id=1, replica_groups={{21,20,9,8,29,28,17,16,5,4,25,24,13,12,1,0},{23,22,11,10,31,30,19,18,7,..., dimensions={0} | all-to-all | bytes 65536 | tf_op jit(solution)/shard_map/all_to_all | solution.py:484
  21.9 0.9 %pose.1 = bf16[3,2,656]{2,1,0:T(2,128)(2,1)} custom-call(s16[16,8,128]{2,1,0:T(8,128)(2,1)S(1)} %all_to_all.10.recv_ref, f32[4,8,128]{2,1,0:T(8,128)S(1)} %get-tuple-element.21.diff_ref, bf16[128,128]{1,0:T(8,128)(2,1)S(1)} %get-tuple-element.22.above_ref, f32[8,128]{1,0:T(8,128)S(1)} %get-tuple-element.23.shift_ref, ...), custom_call_target="tpu_custom_call" | custom-call | tf_op jit(solution)/shard_map/pose/pallas_call | solution.py:553
Async XLA Ops:
  0.0 9.2 %copy-start = (bf16[100,3,82]{0,2,1:T(8,128)(2,1)S(1)}, bf16[100,3,82]{0,2,1:T(8,128)(2,1)}, u32[]{:S(2)}) copy-start(bf16[100,3,82]{0,2,1:T(8,128)(2,1)} %param.10) | copy-start | bytes 147604
  1.5 12.0 %all-to-all-start = ((bf16[16,8,128]{2,1,0:T(8,128)(2,1)}), bf16[16,8,128]{2,1,0:T(8,128)(2,1)S(1)}, u32[]{:S(2)}, u32[]{:S(2)}) async-start(bf16[16,8,128]{2,1,0:T(8,128)(2,1)} %pack.1), calls=%async_computation | async-start | bytes 65536 | tf_op jit(solution)/shard_map/all_to_all | solution.py:484
  9.2 4.4 %collective-permute-start = (bf16[3,82,100]{2,1,0:T(8,128)(2,1)S(1)}, bf16[3,82,100]{2,1,0:T(8,128)(2,1)S(1)}, u32[]{:S(2)}, u32[]{:S(2)}) collective-permute-start(bf16[3,82,100]{2,1,0:T(8,128)(2,1)S(1)} %bitcast.6), channel_id=1, source_target_pairs={{0,2},{1,3},{2,0},{3,1},{4,6},{5,7},{6,4},{7,5},{8,10},{9,11},{10,... | collective-permute-start | bytes 147608 | tf_op jit(solution)/shard_map/ppermute | solution.py:481

commit v9 on v8

--- a/solution.py
+++ b/solution.py
@@ -75,8 +75,8 @@
     return (place + half - 1) % half
 
 
-def order_of(spans, root, stride):
-    return [(root + stride * n) % spans for n in range(spans)]
+def order_of(spans, root):
+    return sorted(range(spans), key=lambda n: (n != root, -abs(n - root), n))
 
 
 def halves(groups, order):
@@ -473,7 +473,7 @@
     members = spans * half
     block = comps // groups
     rows = 2 * own_chars + 2 * slots // half
-    orders = (order_of(spans, spans // 2 - 1, 5), order_of(spans, spans // 2 + 1, 5))
+    orders = (order_of(spans, spans // 2 - 1), order_of(spans, spans // 2 + 1))
     padded = round_up(spans * verts, LANES)
     whole = jax.ShapeDtypeStruct
     room = pltpu.CompilerParams(vmem_limit_bytes=16 * 2**20)

time: 23.1 us -> 23 us (level)
  no operation moved by 1% of the time
where the time goes in v9:
time: 23 us; the launch traced here: 22.8 us
  starting transfers between devices  9.18 us (40%)
  blocking collectives  7.88 us (34%)
  Pallas kernels  4.48 us (19%)
  waiting for transfers between devices  1.19 us (5%)
    all_to_all x1, blocking collectives, exchange(): lax.all_to_all(value, ('vert', 'col'), 0, 0, tiled=True, axis_index_group...  7.88 us
    all_to_all x1, starting transfers between devices, exchange(): lax.all_to_all(value, ('vert', 'col'), 0, 0, tiled=True, axis_index_group...  7.62 us
    pallas_call x1, Pallas kernels, body(): pl.pallas_call(functools.partial(prep_kernel, half), out_shape=[whole((3,...  1.6 us
    ppermute x1, starting transfers between devices, body(): lax.ppermute(basis, 'col', [(n, (n + half) % groups) for n in range(group...  1.56 us
    pallas_call x1, Pallas kernels, body(): pl.pallas_call(functools.partial(pack_kernel, groups, spans), out_shape=w...  1.53 us
    ppermute x1, waiting for transfers between devices, body(): lax.ppermute(basis, 'col', [(n, (n + half) % groups) for n in range(group...  1.19 us
    pallas_call x1, Pallas kernels, body(): pl.pallas_call(functools.partial(pose_kernel, half, orders[1], own_chars,...  0.91 us
  transfers between devices with their start and end apart: 2, of which 1 were waited for; matrix products, arithmetic and copies ran while one was open for 0% of the time, Pallas kernels for 7%

profile of v9, /device:TPU:0, one launch (start us, length us, event | category | flops | bytes accessed | tf_op | source)
XLA Modules:
  0.0 22.8 jit_solution(16845162899534093461)
XLA Ops:
  0.0 0.0 copy-start
  0.0 1.5 %pack.1 = bf16[16,8,128]{2,1,0:T(8,128)(2,1)} custom-call(bf16[2,400]{1,0:T(2,128)(2,1)} %coeffs_hbm.1, s32[4,82]{1,0:T(4,128)} %bitcast.7, f32[4,82]{1,0:T(4,128)} %bitcast.8), custom_call_target="tpu_custom_call" | custom-call | tf_op jit(solution)/shard_map/pack/pallas_call | solution.py:488
  1.5 7.6 %all-to-all-start = ((bf16[16,8,128]{2,1,0:T(8,128)(2,1)}), bf16[16,8,128]{2,1,0:T(8,128)(2,1)S(1)}, u32[]{:S(2)}, u32[]{:S(2)}) async-start(bf16[16,8,128]{2,1,0:T(8,128)(2,1)} %pack.1), calls=%async_computation | async-start | bytes 65536 | tf_op jit(solution)/shard_map/all_to_all | solution.py:484
  9.2 0.0 copy-done
  9.2 1.6 %collective-permute-start = (bf16[3,82,100]{2,1,0:T(8,128)(2,1)S(1)}, bf16[3,82,100]{2,1,0:T(8,128)(2,1)S(1)}, u32[]{:S(2)}, u32[]{:S(2)}) collective-permute-start(bf16[3,82,100]{2,1,0:T(8,128)(2,1)S(1)} %bitcast.6), channel_id=1, source_target_pairs={{0,2},{1,3},{2,0},{3,1},{4,6},{5,7},{6,4},{7,5},{8,10},{9,11},{10,... | collective-permute-start | bytes 147608 | tf_op jit(solution)/shard_map/ppermute | solution.py:481
  10.7 1.6 %prep.1 = (bf16[3,128,128]{2,1,0:T(8,128)(2,1)S(1)}, f32[8,128]{1,0:T(8,128)S(1)}, bf16[256,384]{1,0:T(8,128)(2,1)S(1)}, f32[3,8,128]{2,1,0:T(8,128)S(1)}, f32[4...) custom-call(bf16[3,82,100]{2,1,0:T(8,128)(2,1)} %bitcast.5, f32[3,82]{1,0:T(4,128)} %template_hbm.1, ...), custom_call_target="tpu_custom_call" | custom-call | flops 10000000 | bytes 1000000 | tf_op jit(solution)/shard_map/prep/pallas_call | solution.py:504
  12.3 1.2 %collective-permute-done.other_ref = bf16[3,82,100]{2,1,0:T(8,128)(2,1)S(1)} collective-permute-done((bf16[3,82,100]{2,1,0:T(8,128)(2,1)S(1)}, bf16[3,82,100]{2,1,0:T(8,128)(2,1)S(1)}, u32[]{:S(2)}, u32[]{:S(2)}) %collective-permute-start) | collective-permute-done | bytes 49232 | tf_op jit(solution)/shard_map/ppermute | solution.py:481
  13.5 0.0 all-to-all-done.recv_ref
  13.5 0.4 %shape.1 = (s16[16,8,128]{2,1,0:T(8,128)(2,1)S(1)}, s32[8,768]{1,0:T(8,128)S(1)}, f32[8,768]{1,0:T(8,128)S(1)}, f32[3,8,768]{2,1,0:T(8,128)S(1)}) custom-call(bf16[16,8,128]{2,1,0:T(8,128)(2,1)S(1)} %all-to-all-done.recv_ref, bf16[3,82,100]{2,1,0:T(8,128)(2,1)S(1)} %collective-permute-done.other_ref, bf16[3,128,128]{2,1,0:T(8,128)(2,1)S(1)} %get-tuple-element.16.own_ref, ...), custom_call_target="tpu_custom_call" | custom-call | tf_op jit(solution)/shard_map/shape/pallas_call | solution.py:533
  14.0 7.9 %all_to_all.10.recv_ref = s16[16,8,128]{2,1,0:T(8,128)(2,1)S(1)} all-to-all(s16[16,8,128]{2,1,0:T(8,128)(2,1)S(1)} %get-tuple-element.20), channel_id=1, replica_groups={{21,20,1,0,5,4,9,8,13,12,29,28,17,16,25,24},{23,22,3,2,7,6,11,10,15,14,..., dimensions={0} | all-to-all | bytes 65536 | tf_op jit(solution)/shard_map/all_to_all | solution.py:484
  21.9 0.9 %pose.1 = bf16[3,2,656]{2,1,0:T(2,128)(2,1)} custom-call(s16[16,8,128]{2,1,0:T(8,128)(2,1)S(1)} %all_to_all.10.recv_ref, f32[4,8,128]{2,1,0:T(8,128)S(1)} %get-tuple-element.21.diff_ref, bf16[128,128]{1,0:T(8,128)(2,1)S(1)} %get-tuple-element.22.above_ref, f32[8,128]{1,0:T(8,128)S(1)} %get-tuple-element.23.shift_ref, ...), custom_call_target="tpu_custom_call" | custom-call | tf_op jit(solution)/shard_map/pose/pallas_call | solution.py:553
Async XLA Ops:
  0.0 9.2 %copy-start = (bf16[100,3,82]{0,2,1:T(8,128)(2,1)S(1)}, bf16[100,3,82]{0,2,1:T(8,128)(2,1)}, u32[]{:S(2)}) copy-start(bf16[100,3,82]{0,2,1:T(8,128)(2,1)} %param.10) | copy-start | bytes 147604
  1.5 12.0 %all-to-all-start = ((bf16[16,8,128]{2,1,0:T(8,128)(2,1)}), bf16[16,8,128]{2,1,0:T(8,128)(2,1)S(1)}, u32[]{:S(2)}, u32[]{:S(2)}) async-start(bf16[16,8,128]{2,1,0:T(8,128)(2,1)} %pack.1), calls=%async_computation | async-start | bytes 65536 | tf_op jit(solution)/shard_map/all_to_all | solution.py:484
  9.2 4.4 %collective-permute-start = (bf16[3,82,100]{2,1,0:T(8,128)(2,1)S(1)}, bf16[3,82,100]{2,1,0:T(8,128)(2,1)S(1)}, u32[]{:S(2)}, u32[]{:S(2)}) collective-permute-start(bf16[3,82,100]{2,1,0:T(8,128)(2,1)S(1)} %bitcast.6), channel_id=1, source_target_pairs={{0,2},{1,3},{2,0},{3,1},{4,6},{5,7},{6,4},{7,5},{8,10},{9,11},{10,... | collective-permute-start | bytes 147608 | tf_op jit(solution)/shard_map/ppermute | solution.py:481
